TPU v7x, 32 devices: a whole 2x2x4 slice. The times are simulated.
32 devices in a mesh: keys: 8 (over z, y), view: 4 (over x, core).
Axes of the slice: x: 2, y: 2, z: 4, core: 2. Of those that a mesh axis runs over, the one named last changes fastest.
Arguments:
- key_slot: int32 [4096], replicated, may hold values from 0 to 4095, as said below
- a_slot: int32 [131072], P(('keys', 'view')), may hold values from 0 to 511
- a_group: int32 [131072], P(('keys', 'view')), may hold values from 0 to 1023
- a_weight: int32 [131072], P(('keys', 'view')), may hold values from 1 to 3
- a_payload: bfloat16 [131072, 256], P(('keys', 'view')), may hold values from -1.1953125 to 1.1953125
- b_slot: int32 [131072], P(('keys', 'view')), may hold values from 0 to 511
- b_weight: int32 [131072], P(('keys', 'view')), may hold values from 1 to 3
- b_payload: bfloat16 [131072, 256], P(('keys', 'view')), may hold values from -0.59765625 to 0.59765625
- da_key: int32 [32768], P(('keys', 'view')), may hold values from 0 to 4095, as said below
- da_group: int32 [32768], P(('keys', 'view')), may hold values from 0 to 1023
- da_mult: int32 [32768], P(('keys', 'view')), may hold values from -1 to 1, as said below
- da_payload: bfloat16 [32768, 256], P(('keys', 'view')), may hold values from -1.796875 to 1.796875
- da_count: int32 [32], P(('keys', 'view')), may hold values from 768 to 1024, as said below
- db_key: int32 [32768], P(('keys', 'view')), may hold values from 0 to 4095, as said below
- db_mult: int32 [32768], P(('keys', 'view')), may hold values from -1 to 1, as said below
- db_payload: bfloat16 [32768, 256], P(('keys', 'view')), may hold values from -1.1953125 to 1.1953125
- db_count: int32 [32], P(('keys', 'view')), may hold values from 768 to 1024, as said below
Outputs:
- view_delta: float32 [1024, 256], P(('keys', 'view'))
Inputs may be any that keep to these rules, and one draw needn't show every extreme that they name: `key_slot`: A permutation of 0 to 4095. `da_key`: among the 1024 slots of one device, at most 256 have keys held by one keys index; in every draw one keys index gets exactly 256 live rows from every device. `db_key`: among the 1024 slots of one device, at most 256 have keys held by one keys index; in every draw one keys index gets exactly 256 live rows from every device. `da_mult`: each entry is -1 or 1. `db_mult`: each entry is -1 or 1. `da_count`: some device has all 1024 rows live. `db_count`: some device has all 1024 rows live.
All inputs are finite; a program needn't handle non-finite values.
Results may differ from a plain program's by a relative error of at most 0.0029.
Values may be sent and summed in bfloat16 or wider, within the bound.
A program may use at most 64 MiB of HBM per device.

v0:
```python
import functools
import types

import jax
import jax.numpy as jnp
from jax import lax
from jax.experimental import pallas as pl
from jax.experimental.pallas import tpu as pltpu
from jax.sharding import PartitionSpec as P

LANES = 128
META = 8
F32 = jnp.float32
BF16 = jnp.bfloat16
VMEM_LIMIT = 62 * 1024 * 1024
MARKS_LIMIT = 16 * 1024 * 1024


def row_of(ref, start, count):
    return jnp.concatenate([ref[pl.ds(start + i, 1), :] for i in range(count)], axis=1)


def as_row(ref):
    return row_of(ref, 0, ref.shape[0])


def iota(shape, axis):
    return lax.broadcasted_iota(jnp.int32, shape, axis)


def dot(a, b):
    return jnp.dot(a, b, preferred_element_type=F32)


def hot(mask):
    return jnp.where(mask, 1.0, 0.0).astype(BF16)


def remote(src, dst, send, recv, keys, view):
    return pltpu.make_async_remote_copy(
        src_ref=src, dst_ref=dst, send_sem=send, recv_sem=recv,
        device_id=(keys, view), device_id_type=pl.DeviceIdType.MESH,
    )


def aligned(start, count):
    return pl.ds(pl.multiple_of(start, count), count)


def pack_plan(owners, keys_dev, cap, table_ref, key_ref, mult_ref, group_ref, count):
    key = as_row(key_ref)
    rows = key.shape[1]
    table = table_ref[...]
    tiles = table.shape[0]
    halves = jnp.concatenate([table & 255, table >> 8], axis=0).astype(F32).astype(BF16)
    looked = dot(halves, hot(iota((LANES, rows), 0) == (key & (LANES - 1))))
    high = iota((tiles, rows), 0) == (key >> 7)
    slot_low = jnp.sum(jnp.where(high, looked[:tiles], 0.0), axis=0, keepdims=True)
    slot_high = jnp.sum(jnp.where(high, looked[tiles:], 0.0), axis=0, keepdims=True)
    slot = slot_low.astype(jnp.int32) + 256 * slot_high.astype(jnp.int32)
    owner = slot // keys_dev
    local = slot - owner * keys_dev
    alive = iota((1, rows), 1) < count
    marks = jnp.where((iota((owners, rows), 0) == owner) & alive, 1.0, 0.0)
    step = min(256, rows)
    upper = hot(iota((step, step), 0) < iota((step, step), 1))
    running = jnp.zeros((owners, 1), F32)
    ranks = []
    for at in range(0, rows, step):
        piece = marks[:, at:at + step]
        before = dot(piece.astype(BF16), upper) + running
        ranks.append(jnp.sum(piece * before, axis=0, keepdims=True))
        running = running + jnp.sum(piece, axis=1, keepdims=True)
    rank = jnp.concatenate(ranks, axis=1).astype(jnp.int32)
    dest = jnp.where(alive, owner * cap + rank, -1)
    sign = as_row(mult_ref).astype(F32)
    parts = [local & 255, local >> 8]
    if group_ref is not None:
        group = as_row(group_ref)
        parts += [group & 255, group >> 8]
    meta = jnp.concatenate(
        [p.astype(F32) * sign for p in parts] + [jnp.zeros((META - len(parts), rows), F32)], axis=0
    ).astype(BF16)
    return dest, sign, meta


def packed(plan, cap, pay_ref, owner):
    dest, sign, meta = plan
    place = jnp.where(iota((cap, dest.shape[1]), 0) == dest - owner * cap, sign, 0.0).astype(BF16)
    columns = lax.dot_general(meta, place, (((1,), (1,)), ((), ())), preferred_element_type=F32)
    return dot(place, pay_ref[...]).astype(BF16), columns.astype(BF16)


def put_meta(ref, at, cap, columns):
    lanes = ref.shape[2]
    for t, lane in enumerate(range(0, cap, lanes)):
        wide = min(lanes, cap - lane)
        ref[at, cap + t * META:cap + (t + 1) * META, :wide] = columns[:, lane:lane + wide]


def meta_row(ref, at, row, cap):
    lanes = ref.shape[2]
    found = []
    for r in (row, row + 1):
        pieces = []
        for t, lane in enumerate(range(0, cap, lanes)):
            place = cap + t * META + r
            pieces.append(ref[at, place:place + 1, :min(lanes, cap - lane)].astype(F32))
        found.append(jnp.concatenate(pieces, axis=1).astype(jnp.int32))
    return found[0] + 256 * found[1]


def split(x):
    top = x.astype(BF16)
    return jnp.concatenate([top, (x - top.astype(F32)).astype(BF16)], axis=1)


def columns_of(row, width):
    return jnp.transpose(jnp.broadcast_to(row, (width, row.shape[1])))


def slot_marks(row, weight, keys_dev):
    count = row.shape[1]
    code = columns_of(row * 4 + weight, LANES)
    slot, scale = code >> 2, (code & 3).astype(F32)
    return jnp.concatenate(
        [
            jnp.where(iota((count, LANES), 1) + at == slot, scale, 0.0).astype(BF16)
            for at in range(0, keys_dev, LANES)
        ],
        axis=1,
    )


def kernel(d, *refs):
    (da_count, db_count, key_slot, a_slot, a_weight, a_group, b_slot, b_weight, da_key, da_group, da_mult,
     db_key, db_mult, a_hbm, b_hbm, da_hbm, db_hbm, out) = refs[:18]
    s = types.SimpleNamespace(**dict(zip(d.names, refs[18:], strict=True)))
    n, views, cap, slots, groups, width = d.owners, d.views, d.cap, d.slots, d.groups, d.width
    half, held = width // 2, d.held
    me, view = lax.axis_index("keys"), lax.axis_index("view")
    core = view & 1
    low = n // 2
    side = me // low
    place = me - side * low
    a_rows = s.a_pay.shape[0]

    loads = [
        pltpu.make_async_copy(src, dst, s.load.at[i])
        for i, (src, dst) in enumerate(
            ((db_hbm, s.db_pay), (da_hbm, s.da_pay), (b_hbm, s.b_pay), (a_hbm, s.a_pay))
        )
    ]
    for load in loads:
        load.start()

    barrier = pltpu.get_barrier_semaphore()
    devices = n * views
    mine = me * views + view

    def greet(i, carry):
        other = lax.rem(mine + i, devices)
        pl.semaphore_signal(
            barrier, inc=1, device_id=(other // views, lax.rem(other, views)),
            device_id_type=pl.DeviceIdType.MESH,
        )
        return carry

    lax.fori_loop(1, devices, greet, 0)

    b_plan = pack_plan(n, slots, cap, key_slot, db_key, db_mult, None, db_count[0])
    loads[0].wait()

    def b_pack(low_ref, high_ref, owner):
        rows, columns = packed(b_plan, cap, s.db_pay, owner)
        low_ref[owner, :cap, :] = rows[:, :half]
        high_ref[owner, :cap, :] = rows[:, half:]
        put_meta(low_ref, owner, cap, columns)

    def b_one(i, carry):
        b_pack(s.b_out0, s.b_out1, me ^ i)
        return carry

    lax.fori_loop(1, n, b_one, 0)
    b_pack(s.b_in0, s.b_in1, me)

    def b_copy(j, owner, source):
        src, dst = ((s.b_out0, s.b_in0), (s.b_out1, s.b_in1))[j]
        return remote(src.at[owner], dst.at[source], s.b_send.at[j, owner], s.b_recv.at[j, source], owner, view)

    pl.semaphore_wait(barrier, devices - 1)
    for j in range(2):
        def b_start(i, carry):
            b_copy(j, me ^ (n - i), me).start()
            return carry

        lax.fori_loop(1, n, b_start, 0)

    d_plan = pack_plan(n, slots, cap, key_slot, da_key, da_mult, da_group, da_count[0])
    loads[1].wait()
    from_me = core * low + place

    def d_pack(ref, at, owner):
        rows, columns = packed(d_plan, cap, s.da_pay, owner)
        ref[at, :cap, :] = rows
        put_meta(ref, at, cap, columns)

    def d_copy(owner, source):
        there = owner // low
        return remote(
            s.d_out.at[owner], s.d_in.at[source], s.d_send.at[owner], s.d_recv.at[source],
            side * low + owner - there * low, (view - core) + there,
        )

    def d_one(i, carry):
        owner = from_me ^ (n - i)
        d_pack(s.d_out, owner, owner)
        d_copy(owner, from_me).start()
        return carry

    lax.fori_loop(1, n, d_one, 0)
    d_pack(s.d_in, from_me, from_me)

    def total_steps(part, first, mids, lasts, total, send, recv):
        cut = slots // 2
        keep, give = aligned(core * cut, cut), aligned((1 - core) * cut, cut)
        bits = [1 << b for b in range(1, views.bit_length() - 1)]

        def copy(i):
            if i == 0:
                return remote(part.at[give], first, send.at[0], recv.at[0], me, view ^ 1)
            if i <= len(bits):
                return remote(mids.at[i - 1], lasts.at[i - 1], send.at[i], recv.at[i], me, view ^ bits[i - 1])
            return remote(total.at[keep], total.at[keep], send.at[i], recv.at[i], me, view ^ 1)

        def arrived(i):
            copy(i).wait_recv()
            return part[keep, :] + first[...] if i == 0 else mids[i - 1] + lasts[i - 1]

        def step(i):
            def run():
                if i > len(bits) + 1:
                    copy(i - 1).wait_recv()
                    return
                if 0 < i <= len(bits):
                    mids[i - 1] = arrived(i - 1)
                if i == len(bits) + 1:
                    total[keep, :] = arrived(i - 1)
                copy(i).start()
            return run

        count = len(bits) + 2
        return [step(i) for i in range(count + 1)], [copy(i) for i in range(count)]

    base_steps, base_sent = total_steps(
        s.base, s.base_first, s.base_mid, s.base_last, s.base_total, s.base_send, s.base_recv
    )
    halves = [
        total_steps(
            s.part.at[j], s.part_first.at[j], s.part_mid.at[j], s.part_last.at[j], s.part_total.at[j],
            s.part_send.at[j], s.part_recv.at[j],
        )
        for j in range(2)
    ]

    loads[2].wait()
    chunk = min(1024, s.b_pay.shape[0])
    lines = chunk // LANES
    s.base[...] = jnp.zeros_like(s.base)

    def base_one(c, carry):
        slot = row_of(b_slot, c * lines, lines)
        weight = row_of(b_weight, c * lines, lines).astype(F32)
        marks = jnp.where(iota((slots, chunk), 0) == slot, weight, 0.0).astype(BF16)
        s.base[...] += dot(marks, s.b_pay[aligned(c * chunk, chunk), :])
        return carry

    lax.fori_loop(0, s.b_pay.shape[0] // chunk, base_one, 0)
    base_steps[0]()

    few = min(256, a_rows)
    few_lines = few // LANES

    def slot_one(c, carry):
        s.a_marks[aligned(c * few, few), :] = slot_marks(
            row_of(a_slot, c * few_lines, few_lines), row_of(a_weight, c * few_lines, few_lines), slots
        )
        return carry

    lax.fori_loop(0, a_rows // few, slot_one, 0)
    base_steps[1]()

    block = min(256, groups // 2)
    blocks = groups // 2 // block
    span = min(1024, a_rows)
    span_lines = span // LANES

    def group_ids(g):
        second = g // blocks
        at = iota((block, 1), 0) + (g - second * blocks) * block
        to = at // held
        bit = jnp.where(second == 0, 1 - core, core)
        return (to * 2 + bit) * held + (at - to * held)

    def a_group_marks(g, c):
        return hot(group_ids(g) == row_of(a_group, c * span_lines, span_lines))

    if d.keep:
        def group_one(g, carry):
            for c in range(a_rows // span):
                s.a_groups[aligned(g * block, block), c * span:(c + 1) * span] = a_group_marks(g, c)
            return carry

        lax.fori_loop(0, blocks, group_one, 0)
    for step in base_steps[2:-1]:
        step()
    if d.keep:
        lax.fori_loop(blocks, 2 * blocks, group_one, 0)
    base_steps[-1]()

    def delta_sum(j):
        arrived_at = (s.b_in0, s.b_in1)[j]
        part = s.part.at[j]

        def one(source):
            if j == 0:
                s.b_marks[source] = hot(iota((slots, cap), 0) == meta_row(s.b_in0, source, 0, cap))
            return dot(s.b_marks[source], arrived_at[source, :cap, :])

        part[...] = one(me)

        def step(i, carry):
            source = me ^ (n - i)
            b_copy(j, source, source).wait_recv()
            part[...] += one(source)
            return carry

        lax.fori_loop(1, n, step, 0)

    def a_gather(j):
        s.a_table[...] = split(s.part_total[j])
        lanes = slice(j * half, (j + 1) * half)

        def step(c, carry):
            rows = aligned(c * few, few)
            both = dot(s.a_marks[rows, :], s.a_table[...])
            s.a_terms[rows, lanes] = (
                s.a_pay[rows, lanes].astype(F32) * (both[:, :half] + both[:, half:])
            ).astype(BF16)
            return carry

        lax.fori_loop(0, a_rows // few, step, 0)

    def table_copy(j):
        return remote(s.d_table.at[j], s.d_table.at[j], s.t_send.at[j], s.t_recv.at[j], me ^ low, view)

    def table_send(j):
        @pl.when(core == side)
        def _():
            s.d_table[j] = split(s.part_total[j] + s.base_total[:, j * half:(j + 1) * half])
            table_copy(j).start()

    def d_arrive():
        def one(source):
            s.d_marks[source] = slot_marks(meta_row(s.d_in, source, 0, cap), jnp.ones((1, cap), jnp.int32), slots)
            group = meta_row(s.d_in, source, 2, cap)
            if d.keep:
                def fill(g, carry):
                    s.d_groups[source, aligned(g * block, block), :] = hot(group_ids(g) == group)
                    return carry

                lax.fori_loop(0, 2 * blocks, fill, 0)

        one(from_me)

        def step(i, carry):
            source = from_me ^ (n - i)
            d_copy(source, source).wait_recv()
            one(source)
            return carry

        lax.fori_loop(1, n, step, 0)

    delta_sum(0)
    steps = halves[0][0]
    steps[0]()
    loads[3].wait()
    for step in steps[1:]:
        step()
    table_send(0)
    a_gather(0)
    delta_sum(1)
    steps = halves[1][0]
    steps[0]()
    steps[1]()
    d_arrive()
    for step in steps[2:]:
        step()
    table_send(1)
    a_gather(1)

    def a_sum(g, carry):
        rows = aligned(g * block, block)
        if d.keep:
            s.view[rows, :] = dot(s.a_groups[rows, :], s.a_terms[...])
        else:
            s.view[rows, :] = sum(
                dot(a_group_marks(g, c), s.a_terms[c * span:(c + 1) * span, :]) for c in range(a_rows // span)
            )
        return carry

    lax.fori_loop(0, 2 * blocks, a_sum, 0)

    @pl.when(core != side)
    def _():
        for j in range(2):
            table_copy(j).wait_recv()

    def d_gather(source, carry):
        for j in range(2):
            lanes = slice(j * half, (j + 1) * half)
            both = dot(s.d_marks[source], s.d_table[j])
            s.d_terms[source, :, lanes] = (
                s.d_in[source, :cap, lanes].astype(F32) * (both[:, :half] + both[:, half:])
            ).astype(BF16)
        return carry

    lax.fori_loop(0, n, d_gather, 0)

    def d_sum(g):
        rows = aligned(g * block, block)
        ids = group_ids(g)

        def one(source, total):
            if d.keep:
                marks = s.d_groups[source, rows, :]
            else:
                marks = hot(ids == meta_row(s.d_in, source, 2, cap))
            return total + dot(marks, s.d_terms[source])

        return lax.fori_loop(0, n, one, s.view[rows, :])

    def pair_copy(g):
        rows = aligned(g * block, block)
        return remote(s.give.at[rows], s.take.at[rows], s.p_send.at[g], s.p_recv.at[g], me, view ^ 1)

    def give_one(g, carry):
        s.give[aligned(g * block, block), :] = d_sum(g)
        pair_copy(g).start()
        return carry

    lax.fori_loop(0, blocks, give_one, 0)
    pairs = views // 2
    spot = me * pairs + view // 2
    per = block // held

    def piece_copy(to, source):
        owner = to // pairs
        return remote(
            s.pieces.at[to], s.inbox.at[source], s.o_send.at[to], s.o_recv.at[source],
            owner, (to - owner * pairs) * 2 + core,
        )

    def keep_one(g, carry):
        total = d_sum(g + blocks)
        pair_copy(g).wait_recv()
        total = (total + s.take[aligned(g * block, block), :]).astype(BF16)
        for i in range(per):
            s.pieces[g * per + i] = total[i * held:(i + 1) * held, :]

        def send(i, inner):
            to = g * per + i

            @pl.when(to != spot)
            def _():
                piece_copy(to, spot).start()
            return inner

        lax.fori_loop(0, per, send, 0)
        return carry

    lax.fori_loop(0, blocks, keep_one, 0)
    out[...] = s.pieces[spot].astype(F32)
    everyone = n * pairs

    def collect(i, carry):
        source = lax.rem(spot + i, everyone)
        piece_copy(source, source).wait_recv()
        out[...] += s.inbox[source].astype(F32)
        return carry

    lax.fori_loop(1, everyone, collect, 0)

    def finish(i, carry):
        for j in range(2):
            b_copy(j, me ^ i, me).wait_send()
        d_copy(from_me ^ i, from_me).wait_send()
        return carry

    lax.fori_loop(1, n, finish, 0)
    for sent in base_sent + halves[0][1] + halves[1][1]:
        sent.wait_send()

    @pl.when(core == side)
    def _():
        for j in range(2):
            table_copy(j).wait_send()

    def pair_done(g, carry):
        pair_copy(g).wait_send()
        return carry

    lax.fori_loop(0, blocks, pair_done, 0)

    def piece_done(i, carry):
        piece_copy(lax.rem(spot + i, everyone), spot).wait_send()
        return carry

    lax.fori_loop(1, everyone, piece_done, 0)


def shards(
    groups, key_slot, a_slot, a_group, a_weight, a_payload, b_slot, b_weight, b_payload,
    da_key, da_group, da_mult, da_payload, da_count, db_key, db_mult, db_payload, db_count,
):
    owners, views = lax.axis_size("keys"), lax.axis_size("view")
    a_rows, width = a_payload.shape
    slots = key_slot.shape[0] // owners
    delta = da_payload.shape[0]
    cap = 2 * delta // owners
    half = width // 2
    held = groups // (owners * views)
    bits = max(1, views.bit_length() - 2)
    block = min(256, groups // 2)
    blocks = groups // 2 // block
    keep = 2 * groups * (a_rows + owners * cap) <= MARKS_LIMIT

    def lined(x):
        return x.reshape(-1, LANES)

    def tail(lanes):
        return max(2 * META, META * -(-cap // lanes))

    cut = slots // 2
    dma = pltpu.SemaphoreType.DMA
    scratch = dict(
        a_pay=pltpu.VMEM(a_payload.shape, BF16),
        b_pay=pltpu.VMEM(b_payload.shape, BF16),
        da_pay=pltpu.VMEM(da_payload.shape, BF16),
        db_pay=pltpu.VMEM(db_payload.shape, BF16),
        b_out0=pltpu.VMEM((owners, cap + tail(half), half), BF16),
        b_out1=pltpu.VMEM((owners, cap, half), BF16),
        b_in0=pltpu.VMEM((owners, cap + tail(half), half), BF16),
        b_in1=pltpu.VMEM((owners, cap, half), BF16),
        d_out=pltpu.VMEM((owners, cap + tail(width), width), BF16),
        d_in=pltpu.VMEM((owners, cap + tail(width), width), BF16),
        b_marks=pltpu.VMEM((owners, slots, cap), BF16),
        a_marks=pltpu.VMEM((a_rows, slots), BF16),
        d_marks=pltpu.VMEM((owners, cap, slots), BF16),
        base=pltpu.VMEM((slots, width), F32),
        base_first=pltpu.VMEM((cut, width), F32),
        base_mid=pltpu.VMEM((bits, cut, width), F32),
        base_last=pltpu.VMEM((bits, cut, width), F32),
        base_total=pltpu.VMEM((slots, width), F32),
        part=pltpu.VMEM((2, slots, half), F32),
        part_first=pltpu.VMEM((2, cut, half), F32),
        part_mid=pltpu.VMEM((2, bits, cut, half), F32),
        part_last=pltpu.VMEM((2, bits, cut, half), F32),
        part_total=pltpu.VMEM((2, slots, half), F32),
        a_table=pltpu.VMEM((slots, width), BF16),
        d_table=pltpu.VMEM((2, slots, width), BF16),
        a_terms=pltpu.VMEM((a_rows, width), BF16),
        d_terms=pltpu.VMEM((owners, cap, width), BF16),
        view=pltpu.VMEM((groups, width), F32),
        give=pltpu.VMEM((groups // 2, width), F32),
        take=pltpu.VMEM((groups // 2, width), F32),
        pieces=pltpu.VMEM((owners * views // 2, held, width), BF16),
        inbox=pltpu.VMEM((owners * views // 2, held, width), BF16),
        load=dma((4,)),
        b_send=dma((2, owners)),
        b_recv=dma((2, owners)),
        d_send=dma((owners,)),
        d_recv=dma((owners,)),
        base_send=dma((bits + 2,)),
        base_recv=dma((bits + 2,)),
        part_send=dma((2, bits + 2)),
        part_recv=dma((2, bits + 2)),
        t_send=dma((2,)),
        t_recv=dma((2,)),
        p_send=dma((blocks,)),
        p_recv=dma((blocks,)),
        o_send=dma((owners * views // 2,)),
        o_recv=dma((owners * views // 2,)),
    )
    if keep:
        scratch["a_groups"] = pltpu.VMEM((groups, a_rows), BF16)
        scratch["d_groups"] = pltpu.VMEM((owners, groups, cap), BF16)
    dims = types.SimpleNamespace(
        names=tuple(scratch), owners=owners, views=views, cap=cap, slots=slots, groups=groups, width=width,
        held=held, keep=keep,
    )
    vmem, smem = pl.BlockSpec(memory_space=pltpu.VMEM), pl.BlockSpec(memory_space=pltpu.SMEM)
    away = pl.BlockSpec(memory_space=pl.ANY)
    return pl.pallas_call(
        functools.partial(kernel, dims),
        out_shape=jax.ShapeDtypeStruct((held, width), F32),
        in_specs=[smem] * 2 + [vmem] * 11 + [away] * 4,
        out_specs=vmem,
        scratch_shapes=list(scratch.values()),
        compiler_params=pltpu.CompilerParams(
            collective_id=0, has_side_effects=True, vmem_limit_bytes=VMEM_LIMIT
        ),
        name="delta_view",
    )(
        da_count, db_count, lined(key_slot), lined(a_slot), lined(a_weight), lined(a_group), lined(b_slot),
        lined(b_weight), lined(da_key), lined(da_group), lined(da_mult), lined(db_key), lined(db_mult),
        a_payload, b_payload, da_payload, db_payload,
    )


GROUPS_DEV = 32


def solution(mesh):
    row, wide = P(("keys", "view")), P(("keys", "view"), None)
    groups = GROUPS_DEV * mesh.shape["keys"] * mesh.shape["view"]
    in_specs = (P(), row, row, row, wide, row, row, wide, row, row, row, wide, row, row, row, wide, row)
    return jax.shard_map(
        functools.partial(shards, groups), mesh=mesh, in_specs=in_specs, out_specs=wide, check_vma=False
    )
```

profile of v0, /device:TPU:0, one launch (start us, length us, event | category | flops | bytes accessed | tf_op | source)
XLA Modules:
  0.0 73.7 jit_solution(16341224210606428846)
XLA Ops:
  1.3 71.1 %delta_view.1 = f32[32,256]{1,0:T(8,128)} custom-call(s32[1]{0:T(128)S(6)} %copy.19.refs_0_, s32[1]{0:T(128)S(6)} %copy.20.refs_1_, s32[32,128]{1,0:T(8,128)} %bitcast.11, s32[32,128]{1,0:T(8,128)} %bitcast.12, s32[32,128]{1,0:T(8,128)} %bitcast.13, s32[32,128]{1,0:T(8,128)} %bitcast.14, s32[32,128]{1,0:T(8,128)} %bitcast.15, s32[32,128]{1,0:T(8,128)} %bitcast.16, ...), custom_call_target="tpu_custom_call" | custom-call | tf_op jit(solution)/shard_map/delta_view/pallas_call | solution.py:604
  72.4 1.4 %copy.21 = f32[32,256]{1,0:T(8,128)} copy(f32[32,256]{1,0:T(8,128)} %delta_view.1) | data formatting | bytes 65536
where the time goes:
time: 74 us; the launch traced here: 73.7 us
  Pallas kernels  71.1 us (96%)
  local copies, waits for them, and re-layouts  1.38 us (2%)
  between operations  1.3 us (2%)
    pallas_call x1, Pallas kernels, shards(): pl.pallas_call(functools.partial(kernel, dims), out_shape=jax.ShapeDtypeS...  71.1 us

commit v1 on v0

--- a/solution.py
+++ b/solution.py
@@ -171,97 +171,174 @@
     b_plan = pack_plan(n, slots, cap, key_slot, db_key, db_mult, None, db_count[0])
     loads[0].wait()
 
-    def b_pack(low_ref, high_ref, owner):
-        rows, columns = packed(b_plan, cap, s.db_pay, owner)
-        low_ref[owner, :cap, :] = rows[:, :half]
-        high_ref[owner, :cap, :] = rows[:, half:]
-        put_meta(low_ref, owner, cap, columns)
-
-    def b_one(i, carry):
-        b_pack(s.b_out0, s.b_out1, me ^ i)
-        return carry
-
-    lax.fori_loop(1, n, b_one, 0)
-    b_pack(s.b_in0, s.b_in1, me)
+    from_me = core * low + place
+
+    def row_copy(src, dst, send, recv, owner, source):
+        there = owner // low
+        return remote(
+            src.at[owner], dst.at[source], send.at[owner], recv.at[source],
+            side * low + owner - there * low, (view - core) + there,
+        )
 
     def b_copy(j, owner, source):
         src, dst = ((s.b_out0, s.b_in0), (s.b_out1, s.b_in1))[j]
-        return remote(src.at[owner], dst.at[source], s.b_send.at[j, owner], s.b_recv.at[j, source], owner, view)
-
+        return row_copy(src, dst, s.b_send.at[j], s.b_recv.at[j], owner, source)
+
+    def d_copy(owner, source):
+        return row_copy(s.d_out, s.d_in, s.d_send, s.d_recv, owner, source)
+
+    def b_pack(low_ref, high_ref, at):
+        rows, columns = packed(b_plan, cap, s.db_pay, at)
+        low_ref[at, :cap, :] = rows[:, :half]
+        high_ref[at, :cap, :] = rows[:, half:]
+        put_meta(low_ref, at, cap, columns)
+
+    def b_one(i, carry):
+        b_pack(s.b_out0, s.b_out1, from_me ^ (n - i))
+        return carry
+
+    def b_start(j, i, carry):
+        b_copy(j, from_me ^ (n - i), from_me).start()
+        return carry
+
+    def b_both(i, carry):
+        b_one(i, carry)
+        return b_start(0, i, carry)
+
+    early = min(4, n)
+    lax.fori_loop(1, early, b_one, 0)
     pl.semaphore_wait(barrier, devices - 1)
-    for j in range(2):
-        def b_start(i, carry):
-            b_copy(j, me ^ (n - i), me).start()
-            return carry
-
-        lax.fori_loop(1, n, b_start, 0)
+    lax.fori_loop(1, early, functools.partial(b_start, 0), 0)
+    lax.fori_loop(early, n, b_both, 0)
+    lax.fori_loop(1, n, functools.partial(b_start, 1), 0)
+    b_pack(s.b_in0, s.b_in1, from_me)
 
     d_plan = pack_plan(n, slots, cap, key_slot, da_key, da_mult, da_group, da_count[0])
     loads[1].wait()
-    from_me = core * low + place
-
     def d_pack(ref, at, owner):
         rows, columns = packed(d_plan, cap, s.da_pay, owner)
         ref[at, :cap, :] = rows
         put_meta(ref, at, cap, columns)
 
-    def d_copy(owner, source):
-        there = owner // low
+    step_z = max(1, low // 2)
+
+    def d_fill(i, carry):
+        owner = from_me ^ i
+        d_pack(s.d_out, owner, owner)
+        return carry
+
+    def d_start(i, carry):
+        near = lax.rem(i, step_z)
+        owner = from_me ^ ((i - near) * 2 + step_z + near)
+        d_copy(owner, from_me).start()
+        return carry
+
+    def d_near(i, carry):
+        near = lax.rem(i, step_z)
+        owner = from_me ^ ((i - near) * 2 + near)
+        d_copy(owner, from_me).start()
+        return carry
+
+    lax.fori_loop(1, n, d_fill, 0)
+    lax.fori_loop(1, n // 2, d_near, 0)
+    d_pack(s.d_in, from_me, from_me)
+
+    @pl.when(core == side)
+    def _():
+        lax.fori_loop(0, n // 2, d_start, 0)
+
+    right = core == side
+    wide = views // 2
+    spot_x = view // 2
+    piece = slots // wide
+    own = aligned(spot_x * piece, piece)
+    peers = [lax.rem(spot_x + i, wide) for i in range(1, wide)]
+
+    def wrong(run):
+        pl.when(core != side)(run)
+
+    base_pair = remote(s.base, s.base_first, s.pair_send, s.pair_recv, me, view ^ 1)
+
+    def base_copy(p, source):
+        at = aligned(p * piece, piece)
+        return remote(s.base.at[at], s.base_in.at[source], s.base_send.at[p], s.base_recv.at[source], me, p * 2 + core)
+
+    def base_add():
+        @pl.when(right)
+        def _():
+            base_pair.wait_recv()
+            s.base[...] += s.base_first[...]
+            for p in peers:
+                base_copy(p, spot_x).start()
+
+    def base_end():
+        @pl.when(right)
+        def _():
+            s.base_total[...] = s.base[own, :]
+            for p in peers:
+                base_copy(p, p).wait_recv()
+                s.base_total[...] += s.base_in[p]
+
+    def wide_copy(j, p, source):
+        at = aligned(p * piece, piece)
         return remote(
-            s.d_out.at[owner], s.d_in.at[source], s.d_send.at[owner], s.d_recv.at[source],
-            side * low + owner - there * low, (view - core) + there,
+            s.part.at[j, at], s.part_in.at[j, source], s.w_send.at[j, p], s.w_recv.at[j, source], me, p * 2 + core
         )
 
-    def d_one(i, carry):
-        owner = from_me ^ (n - i)
-        d_pack(s.d_out, owner, owner)
-        d_copy(owner, from_me).start()
-        return carry
-
-    lax.fori_loop(1, n, d_one, 0)
-    d_pack(s.d_in, from_me, from_me)
-
-    def total_steps(part, first, mids, lasts, total, send, recv):
-        cut = slots // 2
-        keep, give = aligned(core * cut, cut), aligned((1 - core) * cut, cut)
-        bits = [1 << b for b in range(1, views.bit_length() - 1)]
-
-        def copy(i):
-            if i == 0:
-                return remote(part.at[give], first, send.at[0], recv.at[0], me, view ^ 1)
-            if i <= len(bits):
-                return remote(mids.at[i - 1], lasts.at[i - 1], send.at[i], recv.at[i], me, view ^ bits[i - 1])
-            return remote(total.at[keep], total.at[keep], send.at[i], recv.at[i], me, view ^ 1)
-
-        def arrived(i):
-            copy(i).wait_recv()
-            return part[keep, :] + first[...] if i == 0 else mids[i - 1] + lasts[i - 1]
-
-        def step(i):
-            def run():
-                if i > len(bits) + 1:
-                    copy(i - 1).wait_recv()
-                    return
-                if 0 < i <= len(bits):
-                    mids[i - 1] = arrived(i - 1)
-                if i == len(bits) + 1:
-                    total[keep, :] = arrived(i - 1)
-                copy(i).start()
-            return run
-
-        count = len(bits) + 2
-        return [step(i) for i in range(count + 1)], [copy(i) for i in range(count)]
-
-    base_steps, base_sent = total_steps(
-        s.base, s.base_first, s.base_mid, s.base_last, s.base_total, s.base_send, s.base_recv
-    )
-    halves = [
-        total_steps(
-            s.part.at[j], s.part_first.at[j], s.part_mid.at[j], s.part_last.at[j], s.part_total.at[j],
-            s.part_send.at[j], s.part_recv.at[j],
-        )
-        for j in range(2)
-    ]
+    def cross_copy(j):
+        return remote(s.part_mid.at[j], s.part_first.at[j], s.x_send.at[j], s.x_recv.at[j], me ^ low, view)
+
+    def total_copy(j, i, source):
+        at = s.part_total.at[j, aligned(source * piece, piece)]
+        return remote(at, at, s.g_send.at[j, i], s.g_recv.at[j, source], me, lax.rem(view + i, views))
+
+    def table_copy(j, source):
+        at = s.d_table.at[j, aligned(source * piece, piece)]
+        return remote(at, at, s.c_send.at[j], s.t_recv.at[j, source], me ^ low, view)
+
+    def table_peer(j, p, source):
+        at = s.d_table.at[j, aligned(source * piece, piece)]
+        return remote(at, at, s.t_send.at[j, p], s.t_recv.at[j, source], me, p * 2 + core)
+
+    def wide_give(j):
+        for p in peers:
+            wide_copy(j, p, spot_x).start()
+
+    def wide_take(j):
+        s.part_mid[j] = s.part[j, own]
+        for p in peers:
+            wide_copy(j, p, p).wait_recv()
+            s.part_mid[j] += s.part_in[j, p]
+        wrong(lambda: cross_copy(j).start())
+
+    def total_give(j):
+        @pl.when(right)
+        def _():
+            cross_copy(j).wait_recv()
+            total = s.part_mid[j] + s.part_first[j]
+            s.part_total[j, own] = total
+            for i in range(1, views):
+                total_copy(j, i, spot_x).start()
+            s.d_table[j, own] = split(total + s.base_total[:, j * half:(j + 1) * half])
+            table_copy(j, spot_x).start()
+            for p in peers:
+                table_peer(j, p, spot_x).start()
+
+    def total_take(j):
+        for p in peers:
+            total_copy(j, 0, p).wait_recv()
+        wrong(lambda: total_copy(j, 0, spot_x).wait_recv())
+
+    def table_relay(j):
+        @wrong
+        def _():
+            table_copy(j, spot_x).wait_recv()
+            for p in peers:
+                table_peer(j, p, spot_x).start()
+
+    def table_take(j):
+        for p in peers:
+            table_peer(j, p, p).wait_recv()
 
     loads[2].wait()
     chunk = min(1024, s.b_pay.shape[0])
@@ -276,9 +353,9 @@
         return carry
 
     lax.fori_loop(0, s.b_pay.shape[0] // chunk, base_one, 0)
-    base_steps[0]()
-
-    few = min(256, a_rows)
+    wrong(base_pair.start)
+
+    few = min(512, a_rows)
     few_lines = few // LANES
 
     def slot_one(c, carry):
@@ -287,89 +364,81 @@
         )
         return carry
 
-    lax.fori_loop(0, a_rows // few, slot_one, 0)
-    base_steps[1]()
-
     block = min(256, groups // 2)
     blocks = groups // 2 // block
     span = min(1024, a_rows)
     span_lines = span // LANES
 
-    def group_ids(g):
-        second = g // blocks
-        at = iota((block, 1), 0) + (g - second * blocks) * block
-        to = at // held
-        bit = jnp.where(second == 0, 1 - core, core)
-        return (to * 2 + bit) * held + (at - to * held)
+    def group_place(group):
+        to = group // held
+        return (to >> 1) * held + group - to * held + jnp.where((to & 1) == core, groups // 2, 0)
+
+    s.a_place[...] = group_place(a_group[...])
+
+    def group_marks(g, count, at):
+        return hot(iota((count, at.shape[1]), 0) + g * count == at)
 
     def a_group_marks(g, c):
-        return hot(group_ids(g) == row_of(a_group, c * span_lines, span_lines))
-
-    if d.keep:
-        def group_one(g, carry):
+        return group_marks(g, block, row_of(s.a_place, c * span_lines, span_lines))
+
+    def a_groups():
+        if not d.keep:
+            return
+
+        def one(g, carry):
             for c in range(a_rows // span):
                 s.a_groups[aligned(g * block, block), c * span:(c + 1) * span] = a_group_marks(g, c)
             return carry
 
-        lax.fori_loop(0, blocks, group_one, 0)
-    for step in base_steps[2:-1]:
-        step()
-    if d.keep:
-        lax.fori_loop(blocks, 2 * blocks, group_one, 0)
-    base_steps[-1]()
+        lax.fori_loop(0, 2 * blocks, one, 0)
 
     def delta_sum(j):
         arrived_at = (s.b_in0, s.b_in1)[j]
-        part = s.part.at[j]
-
-        def one(source):
+
+        def fill(source):
             if j == 0:
-                s.b_marks[source] = hot(iota((slots, cap), 0) == meta_row(s.b_in0, source, 0, cap))
-            return dot(s.b_marks[source], arrived_at[source, :cap, :])
-
-        part[...] = one(me)
+                marks = hot(iota((slots, cap), 0) == meta_row(s.b_in0, source, 0, cap))
+                if d.flat:
+                    s.b_marks[:, aligned(source * cap, cap)] = marks
+                else:
+                    s.b_marks[source] = marks
+
+        fill(from_me)
 
         def step(i, carry):
-            source = me ^ (n - i)
+            source = from_me ^ (n - i)
             b_copy(j, source, source).wait_recv()
-            part[...] += one(source)
+            fill(source)
             return carry
 
         lax.fori_loop(1, n, step, 0)
+        if d.flat:
+            s.part[j] = dot(s.b_marks[...], arrived_at[:, :cap, :].reshape(n * cap, half))
+        else:
+            s.part[j] = lax.fori_loop(
+                0, n, lambda i, total: total + dot(s.b_marks[i], arrived_at[i, :cap, :]), jnp.zeros((slots, half), F32)
+            )
 
     def a_gather(j):
         s.a_table[...] = split(s.part_total[j])
         lanes = slice(j * half, (j + 1) * half)
 
         def step(c, carry):
-            rows = aligned(c * few, few)
+            rows = aligned(c * span, span)
             both = dot(s.a_marks[rows, :], s.a_table[...])
             s.a_terms[rows, lanes] = (
                 s.a_pay[rows, lanes].astype(F32) * (both[:, :half] + both[:, half:])
             ).astype(BF16)
             return carry
 
-        lax.fori_loop(0, a_rows // few, step, 0)
-
-    def table_copy(j):
-        return remote(s.d_table.at[j], s.d_table.at[j], s.t_send.at[j], s.t_recv.at[j], me ^ low, view)
-
-    def table_send(j):
-        @pl.when(core == side)
-        def _():
-            s.d_table[j] = split(s.part_total[j] + s.base_total[:, j * half:(j + 1) * half])
-            table_copy(j).start()
+        lax.fori_loop(0, a_rows // span, step, 0)
 
     def d_arrive():
         def one(source):
-            s.d_marks[source] = slot_marks(meta_row(s.d_in, source, 0, cap), jnp.ones((1, cap), jnp.int32), slots)
-            group = meta_row(s.d_in, source, 2, cap)
+            rows = aligned(source * cap, cap)
+            s.d_marks[rows, :] = slot_marks(meta_row(s.d_in, source, 0, cap), jnp.ones((1, cap), jnp.int32), slots)
             if d.keep:
-                def fill(g, carry):
-                    s.d_groups[source, aligned(g * block, block), :] = hot(group_ids(g) == group)
-                    return carry
-
-                lax.fori_loop(0, 2 * blocks, fill, 0)
+                s.d_groups[:, rows] = group_marks(0, groups, group_place(meta_row(s.d_in, source, 2, cap)))
 
         one(from_me)
 
@@ -382,22 +451,30 @@
         lax.fori_loop(1, n, step, 0)
 
     delta_sum(0)
-    steps = halves[0][0]
-    steps[0]()
+    wide_give(0)
+    base_add()
+    lax.fori_loop(0, a_rows // few, slot_one, 0)
+
+    a_groups()
+    wide_take(0)
+    delta_sum(1)
+    wide_give(1)
+    base_end()
     loads[3].wait()
-    for step in steps[1:]:
-        step()
-    table_send(0)
+    wide_take(1)
+    @wrong
+    def _():
+        lax.fori_loop(0, n // 2, d_start, 0)
+
+    total_give(0)
+    total_take(0)
     a_gather(0)
-    delta_sum(1)
-    steps = halves[1][0]
-    steps[0]()
-    steps[1]()
+    total_give(1)
+    table_relay(0)
     d_arrive()
-    for step in steps[2:]:
-        step()
-    table_send(1)
+    total_take(1)
     a_gather(1)
+    table_relay(1)
 
     def a_sum(g, carry):
         rows = aligned(g * block, block)
@@ -411,32 +488,30 @@
 
     lax.fori_loop(0, 2 * blocks, a_sum, 0)
 
-    @pl.when(core != side)
-    def _():
-        for j in range(2):
-            table_copy(j).wait_recv()
-
-    def d_gather(source, carry):
+    for j in range(2):
+        table_take(j)
+
+    several = min(n, span // cap)
+
+    def d_gather(c, carry):
+        rows = aligned(c * several * cap, several * cap)
         for j in range(2):
             lanes = slice(j * half, (j + 1) * half)
-            both = dot(s.d_marks[source], s.d_table[j])
-            s.d_terms[source, :, lanes] = (
-                s.d_in[source, :cap, lanes].astype(F32) * (both[:, :half] + both[:, half:])
-            ).astype(BF16)
-        return carry
-
-    lax.fori_loop(0, n, d_gather, 0)
+            both = dot(s.d_marks[rows, :], s.d_table[j])
+            pay = s.d_in[pl.ds(c * several, several), :cap, lanes].reshape(several * cap, half)
+            s.d_terms[rows, lanes] = (pay.astype(F32) * (both[:, :half] + both[:, half:])).astype(BF16)
+        return carry
+
+    lax.fori_loop(0, n // several, d_gather, 0)
 
     def d_sum(g):
         rows = aligned(g * block, block)
-        ids = group_ids(g)
+        if d.keep:
+            return s.view[rows, :] + dot(s.d_groups[rows, :], s.d_terms[...])
 
         def one(source, total):
-            if d.keep:
-                marks = s.d_groups[source, rows, :]
-            else:
-                marks = hot(ids == meta_row(s.d_in, source, 2, cap))
-            return total + dot(marks, s.d_terms[source])
+            marks = group_marks(g, block, group_place(meta_row(s.d_in, source, 2, cap)))
+            return total + dot(marks, s.d_terms[aligned(source * cap, cap), :])
 
         return lax.fori_loop(0, n, one, s.view[rows, :])
 
@@ -493,18 +568,31 @@
 
     def finish(i, carry):
         for j in range(2):
-            b_copy(j, me ^ i, me).wait_send()
+            b_copy(j, from_me ^ i, from_me).wait_send()
         d_copy(from_me ^ i, from_me).wait_send()
         return carry
 
     lax.fori_loop(1, n, finish, 0)
-    for sent in base_sent + halves[0][1] + halves[1][1]:
-        sent.wait_send()
-
-    @pl.when(core == side)
+
+    @wrong
     def _():
+        base_pair.wait_send()
         for j in range(2):
-            table_copy(j).wait_send()
+            cross_copy(j).wait_send()
+
+    @pl.when(right)
+    def _():
+        for p in peers:
+            base_copy(p, spot_x).wait_send()
+        for j in range(2):
+            for i in range(1, views):
+                total_copy(j, i, spot_x).wait_send()
+            table_copy(j, spot_x).wait_send()
+
+    for j in range(2):
+        for p in peers:
+            wide_copy(j, p, spot_x).wait_send()
+            table_peer(j, p, spot_x).wait_send()
 
     def pair_done(g, carry):
         pair_copy(g).wait_send()
@@ -530,10 +618,12 @@
     cap = 2 * delta // owners
     half = width // 2
     held = groups // (owners * views)
-    bits = max(1, views.bit_length() - 2)
+    wide = views // 2
+    piece = slots // wide
     block = min(256, groups // 2)
     blocks = groups // 2 // block
-    keep = 2 * groups * (a_rows + owners * cap) <= MARKS_LIMIT
+    flat = cap % LANES == 0
+    keep = flat and 2 * groups * (a_rows + owners * cap) <= MARKS_LIMIT
 
     def lined(x):
         return x.reshape(-1, LANES)
@@ -541,7 +631,6 @@
     def tail(lanes):
         return max(2 * META, META * -(-cap // lanes))
 
-    cut = slots // 2
     dma = pltpu.SemaphoreType.DMA
     scratch = dict(
         a_pay=pltpu.VMEM(a_payload.shape, BF16),
@@ -554,23 +643,23 @@
         b_in1=pltpu.VMEM((owners, cap, half), BF16),
         d_out=pltpu.VMEM((owners, cap + tail(width), width), BF16),
         d_in=pltpu.VMEM((owners, cap + tail(width), width), BF16),
-        b_marks=pltpu.VMEM((owners, slots, cap), BF16),
+        b_marks=pltpu.VMEM((slots, owners * cap) if flat else (owners, slots, cap), BF16),
         a_marks=pltpu.VMEM((a_rows, slots), BF16),
-        d_marks=pltpu.VMEM((owners, cap, slots), BF16),
+        d_marks=pltpu.VMEM((owners * cap, slots), BF16),
         base=pltpu.VMEM((slots, width), F32),
-        base_first=pltpu.VMEM((cut, width), F32),
-        base_mid=pltpu.VMEM((bits, cut, width), F32),
-        base_last=pltpu.VMEM((bits, cut, width), F32),
-        base_total=pltpu.VMEM((slots, width), F32),
+        base_first=pltpu.VMEM((slots, width), F32),
+        base_in=pltpu.VMEM((wide, piece, width), F32),
+        base_total=pltpu.VMEM((piece, width), F32),
         part=pltpu.VMEM((2, slots, half), F32),
-        part_first=pltpu.VMEM((2, cut, half), F32),
-        part_mid=pltpu.VMEM((2, bits, cut, half), F32),
-        part_last=pltpu.VMEM((2, bits, cut, half), F32),
+        part_in=pltpu.VMEM((2, wide, piece, half), F32),
+        part_mid=pltpu.VMEM((2, piece, half), F32),
+        part_first=pltpu.VMEM((2, piece, half), F32),
         part_total=pltpu.VMEM((2, slots, half), F32),
         a_table=pltpu.VMEM((slots, width), BF16),
         d_table=pltpu.VMEM((2, slots, width), BF16),
         a_terms=pltpu.VMEM((a_rows, width), BF16),
-        d_terms=pltpu.VMEM((owners, cap, width), BF16),
+        d_terms=pltpu.VMEM((owners * cap, width), BF16),
+        a_place=pltpu.VMEM((a_rows // LANES, LANES), jnp.int32),
         view=pltpu.VMEM((groups, width), F32),
         give=pltpu.VMEM((groups // 2, width), F32),
         take=pltpu.VMEM((groups // 2, width), F32),
@@ -581,12 +670,19 @@
         b_recv=dma((2, owners)),
         d_send=dma((owners,)),
         d_recv=dma((owners,)),
-        base_send=dma((bits + 2,)),
-        base_recv=dma((bits + 2,)),
-        part_send=dma((2, bits + 2)),
-        part_recv=dma((2, bits + 2)),
-        t_send=dma((2,)),
-        t_recv=dma((2,)),
+        pair_send=dma,
+        pair_recv=dma,
+        base_send=dma((wide,)),
+        base_recv=dma((wide,)),
+        w_send=dma((2, wide)),
+        w_recv=dma((2, wide)),
+        x_send=dma((2,)),
+        x_recv=dma((2,)),
+        g_send=dma((2, views)),
+        g_recv=dma((2, wide)),
+        c_send=dma((2,)),
+        t_send=dma((2, wide)),
+        t_recv=dma((2, wide)),
         p_send=dma((blocks,)),
         p_recv=dma((blocks,)),
         o_send=dma((owners * views // 2,)),
@@ -594,10 +690,10 @@
     )
     if keep:
         scratch["a_groups"] = pltpu.VMEM((groups, a_rows), BF16)
-        scratch["d_groups"] = pltpu.VMEM((owners, groups, cap), BF16)
+        scratch["d_groups"] = pltpu.VMEM((groups, owners * cap), BF16)
     dims = types.SimpleNamespace(
         names=tuple(scratch), owners=owners, views=views, cap=cap, slots=slots, groups=groups, width=width,
-        held=held, keep=keep,
+        held=held, keep=keep, flat=flat,
     )
     vmem, smem = pl.BlockSpec(memory_space=pltpu.VMEM), pl.BlockSpec(memory_space=pltpu.SMEM)
     away = pl.BlockSpec(memory_space=pl.ANY)

time: 74 us -> 61 us (0.82)
  Pallas kernels: 71.1 us -> 58 us
    pallas_call x1, Pallas kernels: 71.1 us -> 58 us  [shards(): pl.pallas_call(functools.partial(kernel, dims), out_shape=jax.ShapeDtypeS...]
where the time goes in v1:
time: 61 us; the launch traced here: 60.7 us
  Pallas kernels  58 us (95%)
  local copies, waits for them, and re-layouts  1.38 us (2%)
  between operations  1.3 us (2%)
    pallas_call x1, Pallas kernels, shards(): pl.pallas_call(functools.partial(kernel, dims), out_shape=jax.ShapeDtypeS...  58 us
    unnamed x1, local copies, waits for them, and re-layouts  1.38 us

profile of v1, /device:TPU:0, one launch (start us, length us, event | category | flops | bytes accessed | tf_op | source)
XLA Modules:
  0.0 60.7 jit_solution(5502948533044377169)
XLA Ops:
  1.3 58.0 %delta_view.1 = f32[32,256]{1,0:T(8,128)} custom-call(s32[1]{0:T(128)S(6)} %copy.19.refs_0_, s32[1]{0:T(128)S(6)} %copy.20.refs_1_, s32[32,128]{1,0:T(8,128)} %bitcast.11, s32[32,128]{1,0:T(8,128)} %bitcast.12, s32[32,128]{1,0:T(8,128)} %bitcast.13, s32[32,128]{1,0:T(8,128)} %bitcast.14, s32[32,128]{1,0:T(8,128)} %bitcast.15, s32[32,128]{1,0:T(8,128)} %bitcast.16, ...), custom_call_target="tpu_custom_call" | custom-call | tf_op jit(solution)/shard_map/delta_view/pallas_call | solution.py:700
  59.3 1.4 %copy.21 = f32[32,256]{1,0:T(8,128)} copy(f32[32,256]{1,0:T(8,128)} %delta_view.1) | data formatting | bytes 65536

commit v2 on v1

--- a/solution.py
+++ b/solution.py
@@ -205,47 +205,13 @@
         b_one(i, carry)
         return b_start(0, i, carry)
 
-    early = min(4, n)
+    early = min(3, n)
     lax.fori_loop(1, early, b_one, 0)
     pl.semaphore_wait(barrier, devices - 1)
     lax.fori_loop(1, early, functools.partial(b_start, 0), 0)
     lax.fori_loop(early, n, b_both, 0)
     lax.fori_loop(1, n, functools.partial(b_start, 1), 0)
     b_pack(s.b_in0, s.b_in1, from_me)
-
-    d_plan = pack_plan(n, slots, cap, key_slot, da_key, da_mult, da_group, da_count[0])
-    loads[1].wait()
-    def d_pack(ref, at, owner):
-        rows, columns = packed(d_plan, cap, s.da_pay, owner)
-        ref[at, :cap, :] = rows
-        put_meta(ref, at, cap, columns)
-
-    step_z = max(1, low // 2)
-
-    def d_fill(i, carry):
-        owner = from_me ^ i
-        d_pack(s.d_out, owner, owner)
-        return carry
-
-    def d_start(i, carry):
-        near = lax.rem(i, step_z)
-        owner = from_me ^ ((i - near) * 2 + step_z + near)
-        d_copy(owner, from_me).start()
-        return carry
-
-    def d_near(i, carry):
-        near = lax.rem(i, step_z)
-        owner = from_me ^ ((i - near) * 2 + near)
-        d_copy(owner, from_me).start()
-        return carry
-
-    lax.fori_loop(1, n, d_fill, 0)
-    lax.fori_loop(1, n // 2, d_near, 0)
-    d_pack(s.d_in, from_me, from_me)
-
-    @pl.when(core == side)
-    def _():
-        lax.fori_loop(0, n // 2, d_start, 0)
 
     right = core == side
     wide = views // 2
@@ -274,71 +240,108 @@
     def base_end():
         @pl.when(right)
         def _():
-            s.base_total[...] = s.base[own, :]
+            s.base_total[own, :] = s.base[own, :]
             for p in peers:
                 base_copy(p, p).wait_recv()
-                s.base_total[...] += s.base_in[p]
-
-    def wide_copy(j, p, source):
-        at = aligned(p * piece, piece)
+                s.base_total[own, :] += s.base_in[p]
+
+    def base_all(p, source):
+        at = s.base_total.at[aligned(source * piece, piece)]
+        return remote(at, at, s.all_send.at[p], s.all_recv.at[source], me, p * 2 + core)
+
+    def base_spread():
+        @pl.when(right)
+        def _():
+            for p in peers:
+                base_all(p, spot_x).start()
+
+    sub = piece // 2
+    subs = [pl.ds(q * sub, sub) for q in range(2)]
+
+    def part_of(p, q):
+        return aligned(p * piece + q * sub, sub)
+
+    def wide_copy(j, p, source, q):
         return remote(
-            s.part.at[j, at], s.part_in.at[j, source], s.w_send.at[j, p], s.w_recv.at[j, source], me, p * 2 + core
+            s.part.at[j, part_of(p, q)], s.part_in.at[j, source, subs[q]],
+            s.w_send.at[j, p, q], s.w_recv.at[j, source, q], me, p * 2 + core,
         )
 
-    def cross_copy(j):
-        return remote(s.part_mid.at[j], s.part_first.at[j], s.x_send.at[j], s.x_recv.at[j], me ^ low, view)
-
-    def total_copy(j, i, source):
-        at = s.part_total.at[j, aligned(source * piece, piece)]
-        return remote(at, at, s.g_send.at[j, i], s.g_recv.at[j, source], me, lax.rem(view + i, views))
-
-    def table_copy(j, source):
-        at = s.d_table.at[j, aligned(source * piece, piece)]
-        return remote(at, at, s.c_send.at[j], s.t_recv.at[j, source], me ^ low, view)
-
-    def table_peer(j, p, source):
-        at = s.d_table.at[j, aligned(source * piece, piece)]
-        return remote(at, at, s.t_send.at[j, p], s.t_recv.at[j, source], me, p * 2 + core)
+    def cross_copy(j, q):
+        return remote(
+            s.part_mid.at[j, subs[q]], s.part_first.at[j, subs[q]], s.x_send.at[j, q], s.x_recv.at[j, q], me ^ low, view
+        )
+
+    def total_copy(j, i, source, q):
+        at = s.part_total.at[j, part_of(source, q)]
+        return remote(at, at, s.g_send.at[j, i, q], s.g_recv.at[j, source, q], me, lax.rem(view + i, views))
+
+    def table_copy(j, source, q):
+        at = s.d_table.at[j, part_of(source, q)]
+        return remote(at, at, s.c_send.at[j, q], s.t_recv.at[j, source, q], me ^ low, view)
+
+    def table_peer(j, p, source, q):
+        at = s.d_table.at[j, part_of(source, q)]
+        return remote(at, at, s.t_send.at[j, p, q], s.t_recv.at[j, source, q], me, p * 2 + core)
 
     def wide_give(j):
-        for p in peers:
-            wide_copy(j, p, spot_x).start()
+        for q in range(2):
+            for p in peers:
+                wide_copy(j, p, spot_x, q).start()
 
     def wide_take(j):
-        s.part_mid[j] = s.part[j, own]
-        for p in peers:
-            wide_copy(j, p, p).wait_recv()
-            s.part_mid[j] += s.part_in[j, p]
-        wrong(lambda: cross_copy(j).start())
+        for q in range(2):
+            total = s.part[j, part_of(spot_x, q)]
+            for p in peers:
+                wide_copy(j, p, p, q).wait_recv()
+                total += s.part_in[j, p, subs[q]]
+            s.part_mid[j, subs[q]] = total
+            wrong(lambda: cross_copy(j, q).start())
 
     def total_give(j):
         @pl.when(right)
         def _():
-            cross_copy(j).wait_recv()
-            total = s.part_mid[j] + s.part_first[j]
-            s.part_total[j, own] = total
-            for i in range(1, views):
-                total_copy(j, i, spot_x).start()
-            s.d_table[j, own] = split(total + s.base_total[:, j * half:(j + 1) * half])
-            table_copy(j, spot_x).start()
+            for q in range(2):
+                cross_copy(j, q).wait_recv()
+                total = s.part_mid[j, subs[q]] + s.part_first[j, subs[q]]
+                s.part_total[j, part_of(spot_x, q)] = total
+                for i in range(1, views):
+                    total_copy(j, i, spot_x, q).start()
+
+    def table_give(j):
+        @pl.when(right)
+        def _():
+            for q in range(2):
+                at = part_of(spot_x, q)
+                s.d_table[j, at] = split(s.part_total[j, at] + s.base_total[at, j * half:(j + 1) * half])
+                table_copy(j, spot_x, q).start()
+
+    def total_take(j):
+        for q in range(2):
             for p in peers:
-                table_peer(j, p, spot_x).start()
-
-    def total_take(j):
-        for p in peers:
-            total_copy(j, 0, p).wait_recv()
-        wrong(lambda: total_copy(j, 0, spot_x).wait_recv())
+                total_copy(j, 0, p, q).wait_recv()
+            wrong(lambda: total_copy(j, 0, spot_x, q).wait_recv())
 
     def table_relay(j):
         @wrong
         def _():
-            table_copy(j, spot_x).wait_recv()
+            for q in range(2):
+                table_copy(j, spot_x, q).wait_recv()
+                for p in peers:
+                    table_peer(j, p, spot_x, q).start()
+
+    def table_take(j):
+        @wrong
+        def _():
+            for q in range(2):
+                for p in peers:
+                    table_peer(j, p, p, q).wait_recv()
+
+        @pl.when(right)
+        def _():
             for p in peers:
-                table_peer(j, p, spot_x).start()
-
-    def table_take(j):
-        for p in peers:
-            table_peer(j, p, p).wait_recv()
+                at = aligned(p * piece, piece)
+                s.d_table[j, at] = split(s.part_total[j, at] + s.base_total[at, j * half:(j + 1) * half])
 
     loads[2].wait()
     chunk = min(1024, s.b_pay.shape[0])
@@ -364,14 +367,49 @@
         )
         return carry
 
+    d_plan = pack_plan(n, slots, cap, key_slot, da_key, da_mult, da_group, da_count[0])
+    loads[1].wait()
+    def d_pack(ref, at, owner):
+        rows, columns = packed(d_plan, cap, s.da_pay, owner)
+        ref[at, :cap, :] = rows
+        put_meta(ref, at, cap, columns)
+
+    step_z = max(1, low // 2)
+
+    def d_fill(i, carry):
+        owner = from_me ^ i
+        d_pack(s.d_out, owner, owner)
+        return carry
+
+    def d_start(i, carry):
+        near = lax.rem(i, step_z)
+        owner = from_me ^ ((i - near) * 2 + step_z + near)
+        d_copy(owner, from_me).start()
+        return carry
+
+    def d_near(i, carry):
+        near = lax.rem(i, step_z)
+        owner = from_me ^ ((i - near) * 2 + near)
+        d_copy(owner, from_me).start()
+        return carry
+
+    lax.fori_loop(1, n, d_fill, 0)
+    lax.fori_loop(1, n // 2, d_near, 0)
+    d_pack(s.d_in, from_me, from_me)
+
+    @pl.when(core == side)
+    def _():
+        lax.fori_loop(0, n // 2, d_start, 0)
+
     block = min(256, groups // 2)
     blocks = groups // 2 // block
-    span = min(1024, a_rows)
+    span = min(2048, a_rows)
     span_lines = span // LANES
 
     def group_place(group):
         to = group // held
-        return (to >> 1) * held + group - to * held + jnp.where((to & 1) == core, groups // 2, 0)
+        turned = (to >> 1) ^ ((1 - side) * (devices // 4))
+        return turned * held + group - to * held + jnp.where((to & 1) == core, groups // 2, 0)
 
     s.a_place[...] = group_place(a_group[...])
 
@@ -403,21 +441,27 @@
                 else:
                     s.b_marks[source] = marks
 
-        fill(from_me)
-
         def step(i, carry):
             source = from_me ^ (n - i)
             b_copy(j, source, source).wait_recv()
             fill(source)
             return carry
 
-        lax.fori_loop(1, n, step, 0)
-        if d.flat:
-            s.part[j] = dot(s.b_marks[...], arrived_at[:, :cap, :].reshape(n * cap, half))
-        else:
-            s.part[j] = lax.fori_loop(
-                0, n, lambda i, total: total + dot(s.b_marks[i], arrived_at[i, :cap, :]), jnp.zeros((slots, half), F32)
+        def gather(of):
+            first = of * low
+            rows = arrived_at[pl.ds(first, low), :cap, :].reshape(low * cap, half)
+            if d.flat:
+                return dot(s.b_marks[:, aligned(first * cap, low * cap)], rows)
+            return lax.fori_loop(
+                first, first + low, lambda i, total: total + dot(s.b_marks[i], arrived_at[i, :cap, :]),
+                jnp.zeros((slots, half), F32),
             )
+
+        lax.fori_loop(1, n - low + 1, step, 0)
+        s.part[j] = gather(1 - core)
+        fill(from_me)
+        lax.fori_loop(n - low + 1, n, step, 0)
+        s.part[j] += gather(core)
 
     def a_gather(j):
         s.a_table[...] = split(s.part_total[j])
@@ -433,32 +477,49 @@
 
         lax.fori_loop(0, a_rows // span, step, 0)
 
-    def d_arrive():
+    def d_arrive(first, last, far):
         def one(source):
             rows = aligned(source * cap, cap)
             s.d_marks[rows, :] = slot_marks(meta_row(s.d_in, source, 0, cap), jnp.ones((1, cap), jnp.int32), slots)
             if d.keep:
                 s.d_groups[:, rows] = group_marks(0, groups, group_place(meta_row(s.d_in, source, 2, cap)))
 
-        one(from_me)
+        if first == 0 and not far:
+            one(from_me)
 
         def step(i, carry):
-            source = from_me ^ (n - i)
+            if far:
+                i = lax.rem(i + jnp.where(core == side, 0, n // 4), n // 2)
+            near = lax.rem(i, step_z)
+            source = from_me ^ ((i - near) * 2 + near + (step_z if far else 0))
             d_copy(source, source).wait_recv()
             one(source)
             return carry
 
-        lax.fori_loop(1, n, step, 0)
-
+        lax.fori_loop(first if far else max(first, 1), last, step, 0)
+
+    def a_sum(first, last):
+        def step(g, carry):
+            rows = aligned(g * block, block)
+            if d.keep:
+                s.view[rows, :] = dot(s.a_groups[rows, :], s.a_terms[...])
+            else:
+                s.view[rows, :] = sum(
+                    dot(a_group_marks(g, c), s.a_terms[c * span:(c + 1) * span, :]) for c in range(a_rows // span)
+                )
+            return carry
+
+        lax.fori_loop(first, last, step, 0)
+
+    base_add()
     delta_sum(0)
     wide_give(0)
-    base_add()
     lax.fori_loop(0, a_rows // few, slot_one, 0)
 
-    a_groups()
-    wide_take(0)
     delta_sum(1)
     wide_give(1)
+    wide_take(0)
+    a_groups()
     base_end()
     loads[3].wait()
     wide_take(1)
@@ -467,26 +528,25 @@
         lax.fori_loop(0, n // 2, d_start, 0)
 
     total_give(0)
+    total_give(1)
+    table_give(0)
+    table_give(1)
+    base_spread()
+    d_arrive(0, n // 2, False)
     total_take(0)
     a_gather(0)
-    total_give(1)
+    total_take(1)
     table_relay(0)
-    d_arrive()
-    total_take(1)
     a_gather(1)
+    a_sum(0, blocks)
     table_relay(1)
-
-    def a_sum(g, carry):
-        rows = aligned(g * block, block)
-        if d.keep:
-            s.view[rows, :] = dot(s.a_groups[rows, :], s.a_terms[...])
-        else:
-            s.view[rows, :] = sum(
-                dot(a_group_marks(g, c), s.a_terms[c * span:(c + 1) * span, :]) for c in range(a_rows // span)
-            )
-        return carry
-
-    lax.fori_loop(0, 2 * blocks, a_sum, 0)
+    a_sum(blocks, 2 * blocks)
+    d_arrive(0, n // 2, True)
+
+    @pl.when(right)
+    def _():
+        for p in peers:
+            base_all(p, p).wait_recv()
 
     for j in range(2):
         table_take(j)
@@ -541,10 +601,10 @@
         pair_copy(g).wait_recv()
         total = (total + s.take[aligned(g * block, block), :]).astype(BF16)
         for i in range(per):
-            s.pieces[g * per + i] = total[i * held:(i + 1) * held, :]
+            s.pieces[(g * per + i) ^ ((1 - side) * (devices // 4))] = total[i * held:(i + 1) * held, :]
 
         def send(i, inner):
-            to = g * per + i
+            to = (g * per + i) ^ ((1 - side) * (devices // 4))
 
             @pl.when(to != spot)
             def _():
@@ -555,13 +615,15 @@
         return carry
 
     lax.fori_loop(0, blocks, keep_one, 0)
-    out[...] = s.pieces[spot].astype(F32)
     everyone = n * pairs
+    out[0] = s.pieces[spot].astype(F32)
+    out[1] = jnp.zeros(out.shape[1:], F32)
 
     def collect(i, carry):
         source = lax.rem(spot + i, everyone)
         piece_copy(source, source).wait_recv()
-        out[...] += s.inbox[source].astype(F32)
+        at = i & 1
+        out[at] += s.inbox[source].astype(F32)
         return carry
 
     lax.fori_loop(1, everyone, collect, 0)
@@ -578,21 +640,26 @@
     def _():
         base_pair.wait_send()
         for j in range(2):
-            cross_copy(j).wait_send()
+            for q in range(2):
+                cross_copy(j, q).wait_send()
+                for p in peers:
+                    table_peer(j, p, spot_x, q).wait_send()
 
     @pl.when(right)
     def _():
         for p in peers:
             base_copy(p, spot_x).wait_send()
+            base_all(p, spot_x).wait_send()
         for j in range(2):
-            for i in range(1, views):
-                total_copy(j, i, spot_x).wait_send()
-            table_copy(j, spot_x).wait_send()
+            for q in range(2):
+                for i in range(1, views):
+                    total_copy(j, i, spot_x, q).wait_send()
+                table_copy(j, spot_x, q).wait_send()
 
     for j in range(2):
-        for p in peers:
-            wide_copy(j, p, spot_x).wait_send()
-            table_peer(j, p, spot_x).wait_send()
+        for q in range(2):
+            for p in peers:
+                wide_copy(j, p, spot_x, q).wait_send()
 
     def pair_done(g, carry):
         pair_copy(g).wait_send()
@@ -649,7 +716,7 @@
         base=pltpu.VMEM((slots, width), F32),
         base_first=pltpu.VMEM((slots, width), F32),
         base_in=pltpu.VMEM((wide, piece, width), F32),
-        base_total=pltpu.VMEM((piece, width), F32),
+        base_total=pltpu.VMEM((slots, width), F32),
         part=pltpu.VMEM((2, slots, half), F32),
         part_in=pltpu.VMEM((2, wide, piece, half), F32),
         part_mid=pltpu.VMEM((2, piece, half), F32),
@@ -674,15 +741,17 @@
         pair_recv=dma,
         base_send=dma((wide,)),
         base_recv=dma((wide,)),
-        w_send=dma((2, wide)),
-        w_recv=dma((2, wide)),
-        x_send=dma((2,)),
-        x_recv=dma((2,)),
-        g_send=dma((2, views)),
-        g_recv=dma((2, wide)),
-        c_send=dma((2,)),
-        t_send=dma((2, wide)),
-        t_recv=dma((2, wide)),
+        all_send=dma((wide,)),
+        all_recv=dma((wide,)),
+        w_send=dma((2, wide, 2)),
+        w_recv=dma((2, wide, 2)),
+        x_send=dma((2, 2)),
+        x_recv=dma((2, 2)),
+        g_send=dma((2, views, 2)),
+        g_recv=dma((2, wide, 2)),
+        c_send=dma((2, 2)),
+        t_send=dma((2, wide, 2)),
+        t_recv=dma((2, wide, 2)),
         p_send=dma((blocks,)),
         p_recv=dma((blocks,)),
         o_send=dma((owners * views // 2,)),
@@ -697,9 +766,9 @@
     )
     vmem, smem = pl.BlockSpec(memory_space=pltpu.VMEM), pl.BlockSpec(memory_space=pltpu.SMEM)
     away = pl.BlockSpec(memory_space=pl.ANY)
-    return pl.pallas_call(
+    sums = pl.pallas_call(
         functools.partial(kernel, dims),
-        out_shape=jax.ShapeDtypeStruct((held, width), F32),
+        out_shape=pltpu.VMEM((2, held, width), F32),
         in_specs=[smem] * 2 + [vmem] * 11 + [away] * 4,
         out_specs=vmem,
         scratch_shapes=list(scratch.values()),
@@ -712,6 +781,7 @@
         lined(b_weight), lined(da_key), lined(da_group), lined(da_mult), lined(db_key), lined(db_mult),
         a_payload, b_payload, da_payload, db_payload,
     )
+    return sums[0] + sums[1]
 
 
 GROUPS_DEV = 32

time: 61 us -> 55 us (0.902)
  Pallas kernels: 58 us -> 52.9 us
  local copies, waits for them, and re-layouts: 1.38 us -> 0 us
  other arithmetic: 0 us -> 0.62 us
    pallas_call x1, Pallas kernels: 58 us -> 52.9 us  [shards(): pl.pallas_call(functools.partial(kernel, dims), out_shape=pltpu.VMEM((2,...]
    unnamed x1 -> x0, local copies, waits for them, and re-layouts: 1.38 us -> none
    add x0 -> x1, other arithmetic: none -> 0.62 us  [shards(): return sums[0] + sums[1]]
where the time goes in v2:
time: 55 us; the launch traced here: 54.8 us
  Pallas kernels  52.9 us (96%)
  between operations  1.3 us (2%)
  other arithmetic  0.62 us (1%)
    pallas_call x1, Pallas kernels, shards(): pl.pallas_call(functools.partial(kernel, dims), out_shape=pltpu.VMEM((2,...  52.9 us

profile of v2, /device:TPU:0, one launch (start us, length us, event | category | flops | bytes accessed | tf_op | source)
XLA Modules:
  0.0 54.8 jit_solution(2767870962362024361)
XLA Ops:
  1.3 52.9 %delta_view.1 = f32[2,32,256]{2,1,0:T(8,128)S(1)} custom-call(s32[1]{0:T(128)S(6)} %copy.18.refs_0_, s32[1]{0:T(128)S(6)} %copy.19.refs_1_, s32[32,128]{1,0:T(8,128)} %bitcast.13, s32[32,128]{1,0:T(8,128)} %bitcast.14, s32[32,128]{1,0:T(8,128)} %bitcast.15, s32[32,128]{1,0:T(8,128)} %bitcast.16, s32[32,128]{1,0:T(8,128)} %bitcast.17, s32[32,128]{1,0:T(8,128)} %bitcast.18, ...), custom_call_target="tpu_custom_call" | custom-call | tf_op jit(solution)/shard_map/delta_view/pallas_call | solution.py:769
  54.2 0.6 %add_bitcast_fusion = f32[32,256]{1,0:T(8,128)} fusion(f32[2,32,256]{2,1,0:T(8,128)S(1)} %delta_view.1), kind=kLoop, calls=%fused_computation | loop fusion | flops 8192 | bytes 98304 | tf_op jit(solution)/shard_map/add | solution.py:784

commit v3 on v2

--- a/solution.py
+++ b/solution.py
@@ -133,8 +133,7 @@
 
 
 def kernel(d, *refs):
-    (da_count, db_count, key_slot, a_slot, a_weight, a_group, b_slot, b_weight, da_key, da_group, da_mult,
-     db_key, db_mult, a_hbm, b_hbm, da_hbm, db_hbm, out) = refs[:18]
+    da_count, db_count, *held_away, a_hbm, b_hbm, da_hbm, db_hbm, out = refs[:18]
     s = types.SimpleNamespace(**dict(zip(d.names, refs[18:], strict=True)))
     n, views, cap, slots, groups, width = d.owners, d.views, d.cap, d.slots, d.groups, d.width
     half, held = width // 2, d.held
@@ -145,14 +144,29 @@
     place = me - side * low
     a_rows = s.a_pay.shape[0]
 
+    groups_of = ((0, s.key_slot), (1, s.db_ints), (2, s.da_ints), (3, s.ab_ints))
+    copies = []
+    for i, to in groups_of:
+        for r in range(to.shape[0]):
+            copies.append(pltpu.make_async_copy(held_away[len(copies)], to.at[r], s.load.at[4 + i]))
     loads = [
         pltpu.make_async_copy(src, dst, s.load.at[i])
         for i, (src, dst) in enumerate(
             ((db_hbm, s.db_pay), (da_hbm, s.da_pay), (b_hbm, s.b_pay), (a_hbm, s.a_pay))
         )
     ]
-    for load in loads:
+    for load in copies[:3] + loads[:1] + copies[3:] + loads[1:]:
         load.start()
+
+    def loaded(i):
+        to = groups_of[i][1]
+        pltpu.make_async_copy(to, to, s.load.at[4 + i]).wait()
+
+    def sent(ref, semaphore):
+        remote(ref, ref, semaphore, semaphore, me, view).wait_send()
+
+    def landed(ref, semaphore):
+        remote(ref, ref, semaphore, semaphore, me, view).wait_recv()
 
     barrier = pltpu.get_barrier_semaphore()
     devices = n * views
@@ -168,7 +182,9 @@
 
     lax.fori_loop(1, devices, greet, 0)
 
-    b_plan = pack_plan(n, slots, cap, key_slot, db_key, db_mult, None, db_count[0])
+    loaded(0)
+    loaded(1)
+    b_plan = pack_plan(n, slots, cap, s.key_slot.at[0], s.db_ints.at[0], s.db_ints.at[1], None, db_count[0])
     loads[0].wait()
 
     from_me = core * low + place
@@ -176,16 +192,17 @@
     def row_copy(src, dst, send, recv, owner, source):
         there = owner // low
         return remote(
-            src.at[owner], dst.at[source], send.at[owner], recv.at[source],
+            src.at[owner], dst.at[source], send, recv,
             side * low + owner - there * low, (view - core) + there,
         )
 
     def b_copy(j, owner, source):
         src, dst = ((s.b_out0, s.b_in0), (s.b_out1, s.b_in1))[j]
-        return row_copy(src, dst, s.b_send.at[j], s.b_recv.at[j], owner, source)
+        recv = s.b_recv.at[source] if j == 0 else s.b_later.at[source // low]
+        return row_copy(src, dst, s.b_send.at[j], recv, owner, source)
 
     def d_copy(owner, source):
-        return row_copy(s.d_out, s.d_in, s.d_send, s.d_recv, owner, source)
+        return row_copy(s.d_out, s.d_in, s.d_send, s.d_recv.at[source], owner, source)
 
     def b_pack(low_ref, high_ref, at):
         rows, columns = packed(b_plan, cap, s.db_pay, at)
@@ -205,7 +222,7 @@
         b_one(i, carry)
         return b_start(0, i, carry)
 
-    early = min(3, n)
+    early = min(2, n)
     lax.fori_loop(1, early, b_one, 0)
     pl.semaphore_wait(barrier, devices - 1)
     lax.fori_loop(1, early, functools.partial(b_start, 0), 0)
@@ -218,42 +235,43 @@
     spot_x = view // 2
     piece = slots // wide
     own = aligned(spot_x * piece, piece)
-    peers = [lax.rem(spot_x + i, wide) for i in range(1, wide)]
+    ahead = [(i - 1, lax.rem(spot_x + i, wide)) for i in range(1, wide)]
+    behind = [(i - 1, lax.rem(spot_x + wide - i, wide)) for i in range(1, wide)]
 
     def wrong(run):
         pl.when(core != side)(run)
 
     base_pair = remote(s.base, s.base_first, s.pair_send, s.pair_recv, me, view ^ 1)
 
-    def base_copy(p, source):
+    def base_copy(i, p):
         at = aligned(p * piece, piece)
-        return remote(s.base.at[at], s.base_in.at[source], s.base_send.at[p], s.base_recv.at[source], me, p * 2 + core)
+        return remote(s.base.at[at], s.base_in.at[i], s.base_send.at[i], s.base_recv.at[i], me, p * 2 + core)
 
     def base_add():
         @pl.when(right)
         def _():
             base_pair.wait_recv()
             s.base[...] += s.base_first[...]
-            for p in peers:
-                base_copy(p, spot_x).start()
+            for i, p in ahead:
+                base_copy(i, p).start()
 
     def base_end():
         @pl.when(right)
         def _():
             s.base_total[own, :] = s.base[own, :]
-            for p in peers:
-                base_copy(p, p).wait_recv()
-                s.base_total[own, :] += s.base_in[p]
-
-    def base_all(p, source):
+            for i, p in behind:
+                base_copy(i, p).wait_recv()
+                s.base_total[own, :] += s.base_in[i]
+
+    def base_all(i, p, source):
         at = s.base_total.at[aligned(source * piece, piece)]
-        return remote(at, at, s.all_send.at[p], s.all_recv.at[source], me, p * 2 + core)
+        return remote(at, at, s.all_send.at[i], s.all_recv.at[i], me, p * 2 + core)
 
     def base_spread():
         @pl.when(right)
         def _():
-            for p in peers:
-                base_all(p, spot_x).start()
+            for i, p in ahead:
+                base_all(i, p, spot_x).start()
 
     sub = piece // 2
     subs = [pl.ds(q * sub, sub) for q in range(2)]
@@ -261,40 +279,42 @@
     def part_of(p, q):
         return aligned(p * piece + q * sub, sub)
 
-    def wide_copy(j, p, source, q):
+    def wide_copy(j, i, p, q):
         return remote(
-            s.part.at[j, part_of(p, q)], s.part_in.at[j, source, subs[q]],
-            s.w_send.at[j, p, q], s.w_recv.at[j, source, q], me, p * 2 + core,
+            s.part.at[j, part_of(p, q)], s.part_in.at[j, i, subs[q]], s.w_send, s.w_recv.at[j, i, q], me, p * 2 + core
         )
 
     def cross_copy(j, q):
         return remote(
-            s.part_mid.at[j, subs[q]], s.part_first.at[j, subs[q]], s.x_send.at[j, q], s.x_recv.at[j, q], me ^ low, view
+            s.part_mid.at[j, subs[q]], s.part_first.at[j, subs[q]], s.x_send, s.x_recv.at[j, q], me ^ low, view
         )
 
-    def total_copy(j, i, source, q):
-        at = s.part_total.at[j, part_of(source, q)]
-        return remote(at, at, s.g_send.at[j, i, q], s.g_recv.at[j, source, q], me, lax.rem(view + i, views))
-
-    def table_copy(j, source, q):
-        at = s.d_table.at[j, part_of(source, q)]
-        return remote(at, at, s.c_send.at[j, q], s.t_recv.at[j, source, q], me ^ low, view)
-
-    def table_peer(j, p, source, q):
-        at = s.d_table.at[j, part_of(source, q)]
-        return remote(at, at, s.t_send.at[j, p, q], s.t_recv.at[j, source, q], me, p * 2 + core)
+    def total_copy(j, i, q):
+        at = s.part_total.at[j, part_of(spot_x, q)]
+        return remote(at, at, s.g_send.at[i - 1], s.g_recv.at[j, spot_x], me, lax.rem(view + i, views))
+
+    def total_landed(j, p):
+        landed(s.part_total.at[j, aligned(p * piece, piece)], s.g_recv.at[j, p])
+
+    def table_copy(j):
+        at = s.d_table.at[j, own]
+        return remote(at, at, s.c_send, s.c_recv.at[j], me ^ low, view)
+
+    def table_peer(j, i, p, source):
+        at = s.d_table.at[j, aligned(source * piece, piece)]
+        return remote(at, at, s.t_send, s.t_recv.at[j, i], me, p * 2 + core)
 
     def wide_give(j):
         for q in range(2):
-            for p in peers:
-                wide_copy(j, p, spot_x, q).start()
+            for i, p in ahead:
+                wide_copy(j, i, p, q).start()
 
     def wide_take(j):
         for q in range(2):
             total = s.part[j, part_of(spot_x, q)]
-            for p in peers:
-                wide_copy(j, p, p, q).wait_recv()
-                total += s.part_in[j, p, subs[q]]
+            for i, p in behind:
+                wide_copy(j, i, p, q).wait_recv()
+                total += s.part_in[j, i, subs[q]]
             s.part_mid[j, subs[q]] = total
             wrong(lambda: cross_copy(j, q).start())
 
@@ -303,54 +323,49 @@
         def _():
             for q in range(2):
                 cross_copy(j, q).wait_recv()
-                total = s.part_mid[j, subs[q]] + s.part_first[j, subs[q]]
-                s.part_total[j, part_of(spot_x, q)] = total
+                s.part_total[j, part_of(spot_x, q)] = s.part_mid[j, subs[q]] + s.part_first[j, subs[q]]
                 for i in range(1, views):
-                    total_copy(j, i, spot_x, q).start()
+                    total_copy(j, i, q).start()
 
     def table_give(j):
         @pl.when(right)
         def _():
-            for q in range(2):
-                at = part_of(spot_x, q)
-                s.d_table[j, at] = split(s.part_total[j, at] + s.base_total[at, j * half:(j + 1) * half])
-                table_copy(j, spot_x, q).start()
+            s.d_table[j, own] = split(s.part_total[j, own] + s.base_total[own, j * half:(j + 1) * half])
+            table_copy(j).start()
 
     def total_take(j):
-        for q in range(2):
-            for p in peers:
-                total_copy(j, 0, p, q).wait_recv()
-            wrong(lambda: total_copy(j, 0, spot_x, q).wait_recv())
+        for _, p in behind:
+            total_landed(j, p)
+        wrong(lambda: total_landed(j, spot_x))
 
     def table_relay(j):
         @wrong
         def _():
-            for q in range(2):
-                table_copy(j, spot_x, q).wait_recv()
-                for p in peers:
-                    table_peer(j, p, spot_x, q).start()
+            table_copy(j).wait_recv()
+            for i, p in ahead:
+                table_peer(j, i, p, spot_x).start()
 
     def table_take(j):
         @wrong
         def _():
-            for q in range(2):
-                for p in peers:
-                    table_peer(j, p, p, q).wait_recv()
+            for i, p in behind:
+                table_peer(j, i, p, p).wait_recv()
 
         @pl.when(right)
         def _():
-            for p in peers:
+            for _, p in behind:
                 at = aligned(p * piece, piece)
                 s.d_table[j, at] = split(s.part_total[j, at] + s.base_total[at, j * half:(j + 1) * half])
 
+    loaded(3)
     loads[2].wait()
     chunk = min(1024, s.b_pay.shape[0])
     lines = chunk // LANES
     s.base[...] = jnp.zeros_like(s.base)
 
     def base_one(c, carry):
-        slot = row_of(b_slot, c * lines, lines)
-        weight = row_of(b_weight, c * lines, lines).astype(F32)
+        slot = row_of(s.ab_ints.at[0], c * lines, lines)
+        weight = row_of(s.ab_ints.at[1], c * lines, lines).astype(F32)
         marks = jnp.where(iota((slots, chunk), 0) == slot, weight, 0.0).astype(BF16)
         s.base[...] += dot(marks, s.b_pay[aligned(c * chunk, chunk), :])
         return carry
@@ -363,11 +378,14 @@
 
     def slot_one(c, carry):
         s.a_marks[aligned(c * few, few), :] = slot_marks(
-            row_of(a_slot, c * few_lines, few_lines), row_of(a_weight, c * few_lines, few_lines), slots
+            row_of(s.ab_ints.at[2], c * few_lines, few_lines), row_of(s.ab_ints.at[3], c * few_lines, few_lines), slots
         )
         return carry
 
-    d_plan = pack_plan(n, slots, cap, key_slot, da_key, da_mult, da_group, da_count[0])
+    loaded(2)
+    d_plan = pack_plan(
+        n, slots, cap, s.key_slot.at[0], s.da_ints.at[0], s.da_ints.at[2], s.da_ints.at[1], da_count[0]
+    )
     loads[1].wait()
     def d_pack(ref, at, owner):
         rows, columns = packed(d_plan, cap, s.da_pay, owner)
@@ -411,7 +429,7 @@
         turned = (to >> 1) ^ ((1 - side) * (devices // 4))
         return turned * held + group - to * held + jnp.where((to & 1) == core, groups // 2, 0)
 
-    s.a_place[...] = group_place(a_group[...])
+    s.a_place[...] = group_place(s.ab_ints[4])
 
     def group_marks(g, count, at):
         return hot(iota((count, at.shape[1]), 0) + g * count == at)
@@ -434,16 +452,15 @@
         arrived_at = (s.b_in0, s.b_in1)[j]
 
         def fill(source):
-            if j == 0:
-                marks = hot(iota((slots, cap), 0) == meta_row(s.b_in0, source, 0, cap))
-                if d.flat:
-                    s.b_marks[:, aligned(source * cap, cap)] = marks
-                else:
-                    s.b_marks[source] = marks
+            marks = hot(iota((slots, cap), 0) == meta_row(s.b_in0, source, 0, cap))
+            if d.flat:
+                s.b_marks[:, aligned(source * cap, cap)] = marks
+            else:
+                s.b_marks[source] = marks
 
         def step(i, carry):
             source = from_me ^ (n - i)
-            b_copy(j, source, source).wait_recv()
+            b_copy(0, source, source).wait_recv()
             fill(source)
             return carry
 
@@ -457,10 +474,16 @@
                 jnp.zeros((slots, half), F32),
             )
 
-        lax.fori_loop(1, n - low + 1, step, 0)
+        if j == 0:
+            lax.fori_loop(1, n - low + 1, step, 0)
+        else:
+            landed(s.b_in1.at[pl.ds(0, low)], s.b_later.at[1 - core])
         s.part[j] = gather(1 - core)
-        fill(from_me)
-        lax.fori_loop(n - low + 1, n, step, 0)
+        if j == 0:
+            fill(from_me)
+            lax.fori_loop(n - low + 1, n, step, 0)
+        else:
+            landed(s.b_in1.at[pl.ds(0, low - 1)], s.b_later.at[core])
         s.part[j] += gather(core)
 
     def a_gather(j):
@@ -525,7 +548,7 @@
     wide_take(1)
     @wrong
     def _():
-        lax.fori_loop(0, n // 2, d_start, 0)
+        lax.fori_loop(0, n // 4, d_start, 0)
 
     total_give(0)
     total_give(1)
@@ -535,18 +558,22 @@
     d_arrive(0, n // 2, False)
     total_take(0)
     a_gather(0)
+    @wrong
+    def _():
+        lax.fori_loop(n // 4, n // 2, d_start, 0)
+
     total_take(1)
-    table_relay(0)
     a_gather(1)
     a_sum(0, blocks)
+    table_relay(0)
+    a_sum(blocks, 2 * blocks)
     table_relay(1)
-    a_sum(blocks, 2 * blocks)
     d_arrive(0, n // 2, True)
 
     @pl.when(right)
     def _():
-        for p in peers:
-            base_all(p, p).wait_recv()
+        for i, p in behind:
+            base_all(i, p, p).wait_recv()
 
     for j in range(2):
         table_take(j)
@@ -577,7 +604,7 @@
 
     def pair_copy(g):
         rows = aligned(g * block, block)
-        return remote(s.give.at[rows], s.take.at[rows], s.p_send.at[g], s.p_recv.at[g], me, view ^ 1)
+        return remote(s.give.at[rows], s.take.at[rows], s.p_send, s.p_recv.at[g], me, view ^ 1)
 
     def give_one(g, carry):
         s.give[aligned(g * block, block), :] = d_sum(g)
@@ -592,7 +619,7 @@
     def piece_copy(to, source):
         owner = to // pairs
         return remote(
-            s.pieces.at[to], s.inbox.at[source], s.o_send.at[to], s.o_recv.at[source],
+            s.pieces.at[to], s.inbox.at[source], s.o_send, s.o_recv,
             owner, (to - owner * pairs) * 2 + core,
         )
 
@@ -616,62 +643,35 @@
 
     lax.fori_loop(0, blocks, keep_one, 0)
     everyone = n * pairs
-    out[0] = s.pieces[spot].astype(F32)
-    out[1] = jnp.zeros(out.shape[1:], F32)
-
-    def collect(i, carry):
-        source = lax.rem(spot + i, everyone)
-        piece_copy(source, source).wait_recv()
-        at = i & 1
-        out[at] += s.inbox[source].astype(F32)
-        return carry
-
-    lax.fori_loop(1, everyone, collect, 0)
-
-    def finish(i, carry):
-        for j in range(2):
-            b_copy(j, from_me ^ i, from_me).wait_send()
-        d_copy(from_me ^ i, from_me).wait_send()
-        return carry
-
-    lax.fori_loop(1, n, finish, 0)
+    others = pl.ds(0, everyone - 1)
+    s.inbox[spot] = s.pieces[spot]
+    landed(s.inbox.at[others], s.o_recv)
+    middle = everyone // 2
+    out[0] = jnp.sum(s.inbox[:middle].astype(F32), axis=0)
+    out[1] = jnp.sum(s.inbox[middle:].astype(F32), axis=0)
+
+    rest = pl.ds(0, n - 1)
+    sent(s.b_out0.at[rest], s.b_send.at[0])
+    sent(s.b_out1.at[rest], s.b_send.at[1])
+    sent(s.d_out.at[rest], s.d_send)
+    sent(s.give, s.p_send)
+    sent(s.pieces.at[others], s.o_send)
+    sent(s.part.at[:, pl.ds(0, (wide - 1) * piece)], s.w_send)
 
     @wrong
     def _():
         base_pair.wait_send()
-        for j in range(2):
-            for q in range(2):
-                cross_copy(j, q).wait_send()
-                for p in peers:
-                    table_peer(j, p, spot_x, q).wait_send()
+        sent(s.part_mid, s.x_send)
+        sent(s.d_table.at[:, pl.ds(0, (wide - 1) * piece)], s.t_send)
 
     @pl.when(right)
     def _():
-        for p in peers:
-            base_copy(p, spot_x).wait_send()
-            base_all(p, spot_x).wait_send()
-        for j in range(2):
-            for q in range(2):
-                for i in range(1, views):
-                    total_copy(j, i, spot_x, q).wait_send()
-                table_copy(j, spot_x, q).wait_send()
-
-    for j in range(2):
-        for q in range(2):
-            for p in peers:
-                wide_copy(j, p, spot_x, q).wait_send()
-
-    def pair_done(g, carry):
-        pair_copy(g).wait_send()
-        return carry
-
-    lax.fori_loop(0, blocks, pair_done, 0)
-
-    def piece_done(i, carry):
-        piece_copy(lax.rem(spot + i, everyone), spot).wait_send()
-        return carry
-
-    lax.fori_loop(1, everyone, piece_done, 0)
+        for i, p in ahead:
+            base_copy(i, p).wait_send()
+            base_all(i, p, spot_x).wait_send()
+        for i in range(views - 1):
+            sent(s.part_mid, s.g_send.at[i])
+        sent(s.d_table.at[:, own], s.c_send)
 
 
 def shards(
@@ -699,7 +699,15 @@
         return max(2 * META, META * -(-cap // lanes))
 
     dma = pltpu.SemaphoreType.DMA
+    ints = [
+        lined(x)
+        for x in (key_slot, db_key, db_mult, da_key, da_group, da_mult, b_slot, b_weight, a_slot, a_weight, a_group)
+    ]
     scratch = dict(
+        key_slot=pltpu.VMEM((1, *ints[0].shape), jnp.int32),
+        db_ints=pltpu.VMEM((2, *ints[1].shape), jnp.int32),
+        da_ints=pltpu.VMEM((3, *ints[3].shape), jnp.int32),
+        ab_ints=pltpu.VMEM((5, *ints[6].shape), jnp.int32),
         a_pay=pltpu.VMEM(a_payload.shape, BF16),
         b_pay=pltpu.VMEM(b_payload.shape, BF16),
         da_pay=pltpu.VMEM(da_payload.shape, BF16),
@@ -715,10 +723,10 @@
         d_marks=pltpu.VMEM((owners * cap, slots), BF16),
         base=pltpu.VMEM((slots, width), F32),
         base_first=pltpu.VMEM((slots, width), F32),
-        base_in=pltpu.VMEM((wide, piece, width), F32),
+        base_in=pltpu.VMEM((wide - 1, piece, width), F32),
         base_total=pltpu.VMEM((slots, width), F32),
         part=pltpu.VMEM((2, slots, half), F32),
-        part_in=pltpu.VMEM((2, wide, piece, half), F32),
+        part_in=pltpu.VMEM((2, wide - 1, piece, half), F32),
         part_mid=pltpu.VMEM((2, piece, half), F32),
         part_first=pltpu.VMEM((2, piece, half), F32),
         part_total=pltpu.VMEM((2, slots, half), F32),
@@ -732,30 +740,32 @@
         take=pltpu.VMEM((groups // 2, width), F32),
         pieces=pltpu.VMEM((owners * views // 2, held, width), BF16),
         inbox=pltpu.VMEM((owners * views // 2, held, width), BF16),
-        load=dma((4,)),
-        b_send=dma((2, owners)),
-        b_recv=dma((2, owners)),
-        d_send=dma((owners,)),
+        load=dma((8,)),
+        b_send=dma((2,)),
+        b_recv=dma((owners,)),
+        b_later=dma((2,)),
+        d_send=dma,
         d_recv=dma((owners,)),
         pair_send=dma,
         pair_recv=dma,
-        base_send=dma((wide,)),
-        base_recv=dma((wide,)),
-        all_send=dma((wide,)),
-        all_recv=dma((wide,)),
-        w_send=dma((2, wide, 2)),
-        w_recv=dma((2, wide, 2)),
-        x_send=dma((2, 2)),
+        base_send=dma((wide - 1,)),
+        base_recv=dma((wide - 1,)),
+        all_send=dma((wide - 1,)),
+        all_recv=dma((wide - 1,)),
+        w_send=dma,
+        w_recv=dma((2, wide - 1, 2)),
+        x_send=dma,
         x_recv=dma((2, 2)),
-        g_send=dma((2, views, 2)),
-        g_recv=dma((2, wide, 2)),
-        c_send=dma((2, 2)),
-        t_send=dma((2, wide, 2)),
-        t_recv=dma((2, wide, 2)),
-        p_send=dma((blocks,)),
+        g_send=dma((views - 1,)),
+        g_recv=dma((2, wide)),
+        c_send=dma,
+        c_recv=dma((2,)),
+        t_send=dma,
+        t_recv=dma((2, wide - 1)),
+        p_send=dma,
         p_recv=dma((blocks,)),
-        o_send=dma((owners * views // 2,)),
-        o_recv=dma((owners * views // 2,)),
+        o_send=dma,
+        o_recv=dma,
     )
     if keep:
         scratch["a_groups"] = pltpu.VMEM((groups, a_rows), BF16)
@@ -769,7 +779,7 @@
     sums = pl.pallas_call(
         functools.partial(kernel, dims),
         out_shape=pltpu.VMEM((2, held, width), F32),
-        in_specs=[smem] * 2 + [vmem] * 11 + [away] * 4,
+        in_specs=[smem] * 2 + [away] * 15,
         out_specs=vmem,
         scratch_shapes=list(scratch.values()),
         compiler_params=pltpu.CompilerParams(
@@ -777,8 +787,7 @@
         ),
         name="delta_view",
     )(
-        da_count, db_count, lined(key_slot), lined(a_slot), lined(a_weight), lined(a_group), lined(b_slot),
-        lined(b_weight), lined(da_key), lined(da_group), lined(da_mult), lined(db_key), lined(db_mult),
+        da_count, db_count, *ints,
         a_payload, b_payload, da_payload, db_payload,
     )
     return sums[0] + sums[1]

time: 55 us -> 53.6 us (0.975)
  Pallas kernels: 52.9 us -> 51.3 us
    pallas_call x1, Pallas kernels: 52.9 us -> 51.3 us  [shards(): pl.pallas_call(functools.partial(kernel, dims), out_shape=pltpu.VMEM((2,...]
where the time goes in v3:
time: 53.6 us; the launch traced here: 53.2 us
  Pallas kernels  51.3 us (96%)
  between operations  1.3 us (2%)
  other arithmetic  0.62 us (1%)
    pallas_call x1, Pallas kernels, shards(): pl.pallas_call(functools.partial(kernel, dims), out_shape=pltpu.VMEM((2,...  51.3 us

profile of v3, /device:TPU:0, one launch (start us, length us, event | category | flops | bytes accessed | tf_op | source)
XLA Modules:
  0.0 53.2 jit_solution(2192026948213694716)
XLA Ops:
  1.3 51.3 %delta_view.1 = f32[2,32,256]{2,1,0:T(8,128)S(1)} custom-call(s32[1]{0:T(128)S(6)} %copy.18.refs_0_, s32[1]{0:T(128)S(6)} %copy.19.refs_1_, s32[32,128]{1,0:T(8,128)} %bitcast.13, s32[8,128]{1,0:T(8,128)} %bitcast.19, s32[8,128]{1,0:T(8,128)} %bitcast.20, s32[8,128]{1,0:T(8,128)} %bitcast.21, s32[8,128]{1,0:T(8,128)} %bitcast.22, s32[8,128]{1,0:T(8,128)} %bitcast.23, ...), custom_call_target="tpu_custom_call" | custom-call | tf_op jit(solution)/shard_map/delta_view/pallas_call | solution.py:779
  52.6 0.6 %add_bitcast_fusion = f32[32,256]{1,0:T(8,128)} fusion(f32[2,32,256]{2,1,0:T(8,128)S(1)} %delta_view.1), kind=kLoop, calls=%fused_computation | loop fusion | flops 8192 | bytes 98304 | tf_op jit(solution)/shard_map/add | solution.py:793

commit v4 on v3

--- a/solution.py
+++ b/solution.py
@@ -326,12 +326,12 @@
                 s.part_total[j, part_of(spot_x, q)] = s.part_mid[j, subs[q]] + s.part_first[j, subs[q]]
                 for i in range(1, views):
                     total_copy(j, i, q).start()
+                if j == 1:
+                    table_give(q)
 
     def table_give(j):
-        @pl.when(right)
-        def _():
-            s.d_table[j, own] = split(s.part_total[j, own] + s.base_total[own, j * half:(j + 1) * half])
-            table_copy(j).start()
+        s.d_table[j, own] = split(s.part_total[j, own] + s.base_total[own, j * half:(j + 1) * half])
+        table_copy(j).start()
 
     def total_take(j):
         for _, p in behind:
@@ -498,7 +498,7 @@
             ).astype(BF16)
             return carry
 
-        lax.fori_loop(0, a_rows // span, step, 0)
+        lax.fori_loop(0, a_rows // span, step, 0, unroll=True)
 
     def d_arrive(first, last, far):
         def one(source):
@@ -532,28 +532,26 @@
                 )
             return carry
 
-        lax.fori_loop(first, last, step, 0)
-
-    base_add()
+        lax.fori_loop(first, last, step, 0, unroll=True)
+
     delta_sum(0)
     wide_give(0)
     lax.fori_loop(0, a_rows // few, slot_one, 0)
 
     delta_sum(1)
     wide_give(1)
+    base_add()
     wide_take(0)
     a_groups()
-    base_end()
-    loads[3].wait()
     wide_take(1)
     @wrong
     def _():
         lax.fori_loop(0, n // 4, d_start, 0)
 
     total_give(0)
+    base_end()
+    loads[3].wait()
     total_give(1)
-    table_give(0)
-    table_give(1)
     base_spread()
     d_arrive(0, n // 2, False)
     total_take(0)
@@ -562,21 +560,19 @@
     def _():
         lax.fori_loop(n // 4, n // 2, d_start, 0)
 
+    d_arrive(0, n // 4, True)
     total_take(1)
     a_gather(1)
+    table_relay(0)
     a_sum(0, blocks)
-    table_relay(0)
+    table_relay(1)
     a_sum(blocks, 2 * blocks)
-    table_relay(1)
-    d_arrive(0, n // 2, True)
+    d_arrive(n // 4, n // 2, True)
 
     @pl.when(right)
     def _():
         for i, p in behind:
             base_all(i, p, p).wait_recv()
-
-    for j in range(2):
-        table_take(j)
 
     several = min(n, span // cap)
 
@@ -589,6 +585,8 @@
             s.d_terms[rows, lanes] = (pay.astype(F32) * (both[:, :half] + both[:, half:])).astype(BF16)
         return carry
 
+    table_take(0)
+    table_take(1)
     lax.fori_loop(0, n // several, d_gather, 0)
 
     def d_sum(g):

time: 53.6 us -> 52.5 us (0.979)
  Pallas kernels: 51.3 us -> 49.9 us
    pallas_call x1, Pallas kernels: 51.3 us -> 49.9 us  [shards(): pl.pallas_call(functools.partial(kernel, dims), out_shape=pltpu.VMEM((2,...]
where the time goes in v4:
time: 52.5 us; the launch traced here: 51.9 us
  Pallas kernels  49.9 us (95%)
  between operations  1.3 us (2%)
  other arithmetic  0.62 us (1%)
    pallas_call x1, Pallas kernels, shards(): pl.pallas_call(functools.partial(kernel, dims), out_shape=pltpu.VMEM((2,...  49.9 us

profile of v4, /device:TPU:0, one launch (start us, length us, event | category | flops | bytes accessed | tf_op | source)
XLA Modules:
  0.0 51.9 jit_solution(9939733247574117844)
XLA Ops:
  1.3 49.9 %delta_view.1 = f32[2,32,256]{2,1,0:T(8,128)S(1)} custom-call(s32[1]{0:T(128)S(6)} %copy.18.refs_0_, s32[1]{0:T(128)S(6)} %copy.19.refs_1_, s32[32,128]{1,0:T(8,128)} %bitcast.13, s32[8,128]{1,0:T(8,128)} %bitcast.19, s32[8,128]{1,0:T(8,128)} %bitcast.20, s32[8,128]{1,0:T(8,128)} %bitcast.21, s32[8,128]{1,0:T(8,128)} %bitcast.22, s32[8,128]{1,0:T(8,128)} %bitcast.23, ...), custom_call_target="tpu_custom_call" | custom-call | tf_op jit(solution)/shard_map/delta_view/pallas_call | solution.py:777
  51.2 0.6 %add_bitcast_fusion = f32[32,256]{1,0:T(8,128)} fusion(f32[2,32,256]{2,1,0:T(8,128)S(1)} %delta_view.1), kind=kLoop, calls=%fused_computation | loop fusion | flops 8192 | bytes 98304 | tf_op jit(solution)/shard_map/add | solution.py:791

commit v5 on v4

--- a/solution.py
+++ b/solution.py
@@ -297,11 +297,11 @@
         landed(s.part_total.at[j, aligned(p * piece, piece)], s.g_recv.at[j, p])
 
     def table_copy(j):
-        at = s.d_table.at[j, own]
+        at = s.d_table.at[j, own, pl.ds(0, half)]
         return remote(at, at, s.c_send, s.c_recv.at[j], me ^ low, view)
 
     def table_peer(j, i, p, source):
-        at = s.d_table.at[j, aligned(source * piece, piece)]
+        at = s.d_table.at[j, aligned(source * piece, piece), pl.ds(0, half)]
         return remote(at, at, s.t_send, s.t_recv.at[j, i], me, p * 2 + core)
 
     def wide_give(j):
@@ -549,6 +549,11 @@
         lax.fori_loop(0, n // 4, d_start, 0)
 
     total_give(0)
+    @wrong
+    def _():
+        for j in range(2):
+            s.d_table[j, :, half:] = jnp.zeros((slots, half), BF16)
+
     base_end()
     loads[3].wait()
     total_give(1)
@@ -660,7 +665,7 @@
     def _():
         base_pair.wait_send()
         sent(s.part_mid, s.x_send)
-        sent(s.d_table.at[:, pl.ds(0, (wide - 1) * piece)], s.t_send)
+        sent(s.d_table.at[:, pl.ds(0, (wide - 1) * piece), pl.ds(0, half)], s.t_send)
 
     @pl.when(right)
     def _():
@@ -669,7 +674,7 @@
             base_all(i, p, spot_x).wait_send()
         for i in range(views - 1):
             sent(s.part_mid, s.g_send.at[i])
-        sent(s.d_table.at[:, own], s.c_send)
+        sent(s.d_table.at[:, own, pl.ds(0, half)], s.c_send)
 
 
 def shards(

time: 52.5 us -> 50.7 us (0.966)
  Pallas kernels: 49.9 us -> 48.6 us
    pallas_call x1, Pallas kernels: 49.9 us -> 48.6 us  [shards(): pl.pallas_call(functools.partial(kernel, dims), out_shape=pltpu.VMEM((2,...]
where the time goes in v5:
time: 50.7 us; the launch traced here: 50.5 us
  Pallas kernels  48.6 us (96%)
  between operations  1.3 us (3%)
  other arithmetic  0.62 us (1%)
    pallas_call x1, Pallas kernels, shards(): pl.pallas_call(functools.partial(kernel, dims), out_shape=pltpu.VMEM((2,...  48.6 us

profile of v5, /device:TPU:0, one launch (start us, length us, event | category | flops | bytes accessed | tf_op | source)
XLA Modules:
  0.0 50.5 jit_solution(2273735134339700410)
XLA Ops:
  1.3 48.6 %delta_view.1 = f32[2,32,256]{2,1,0:T(8,128)S(1)} custom-call(s32[1]{0:T(128)S(6)} %copy.18.refs_0_, s32[1]{0:T(128)S(6)} %copy.19.refs_1_, s32[32,128]{1,0:T(8,128)} %bitcast.13, s32[8,128]{1,0:T(8,128)} %bitcast.19, s32[8,128]{1,0:T(8,128)} %bitcast.20, s32[8,128]{1,0:T(8,128)} %bitcast.21, s32[8,128]{1,0:T(8,128)} %bitcast.22, s32[8,128]{1,0:T(8,128)} %bitcast.23, ...), custom_call_target="tpu_custom_call" | custom-call | tf_op jit(solution)/shard_map/delta_view/pallas_call | solution.py:782
  49.9 0.6 %add_bitcast_fusion = f32[32,256]{1,0:T(8,128)} fusion(f32[2,32,256]{2,1,0:T(8,128)S(1)} %delta_view.1), kind=kLoop, calls=%fused_computation | loop fusion | flops 8192 | bytes 98304 | tf_op jit(solution)/shard_map/add | solution.py:796
